TPU v7x, 32 devices: a whole 2x2x4 slice. The times are simulated.
32 devices in a mesh: src: 4 (over z), tile: 8 (over y, x, core).
Axes of the slice: x: 2, y: 2, z: 4, core: 2. Of those that a mesh axis runs over, the one named last changes fastest.
Arguments:
- tables: float32 [32, 32, 32, 1024], P(('src', 'tile')), may hold values from 0.2 to 2
- weights: float32 [32, 32], P(('src', 'tile')), may hold values from 0.05 to 0.5
- aperture: int32 [32, 32], P(('src', 'tile')), may hold values from 0 to 1, as said below
Outputs:
- image: float32 [32, 64, 32, 128], P('tile', 'src')
Inputs may be any that keep to these rules, and one draw needn't show every extreme that they name: `aperture`: within one source and one group of 4 consecutive tiles (g * 4 to g * 4 + 3), at most 2 entries are 1; some group has exactly 2 for every source.
All inputs are finite; a program needn't handle non-finite values.
Results may differ from a plain program's by a relative error of at most 0.0003.
Values sent between devices are 32-bit elements; how exact they have to be, the bound alone decides.
No kernel may reach another device: no remote copies, remote signals or barrier semaphores. Data moves between devices by JAX's collectives and lax.ppermute only.
A program may use at most 128 MiB of HBM per device.

v0:
```python
import jax
import jax.numpy as jnp
from jax import lax
from jax.sharding import PartitionSpec as P

BX = 32
BY = 16
BZ = 64


angular_rate = 9.0


def refine_axis(values, axis):
    length = values.shape[axis]
    first = lax.slice_in_dim(values, 0, 1, axis=axis)
    last = lax.slice_in_dim(values, length - 1, length, axis=axis)
    lower = jnp.concatenate([first, lax.slice_in_dim(values, 0, length - 1, axis=axis)], axis=axis)
    upper = jnp.concatenate([lax.slice_in_dim(values, 1, length, axis=axis), last], axis=axis)
    even_rows = 0.75 * values + 0.25 * lower
    odd_rows = 0.75 * values + 0.25 * upper
    paired = jnp.stack([even_rows, odd_rows], axis=axis + 1)
    shape = values.shape[:axis] + (2 * length,) + values.shape[axis + 1 :]
    return paired.reshape(shape)


def refine_accumulate(coarse, details, fine_rows, tile_count):
    items = coarse.shape[0]
    turns = 8
    block = items // turns
    coarse_rows = coarse.shape[1]
    tile_ids = jnp.arange(tile_count).astype(jnp.float32)

    def one_block(total, item):
        bricks, info = item
        shaped = bricks.reshape(block, coarse_rows, BY, BZ)
        along_x = refine_axis(shaped, 1)
        along_z = refine_axis(along_x, 3)
        fine = refine_axis(along_z, 2)
        phase = jnp.cos(angular_rate * fine)
        select = (info[:, 1:2] == tile_ids[None, :]).astype(jnp.float32) * info[:, 0:1]
        total = total + jnp.einsum("kp,kfyz->pfyz", select, phase, precision=lax.Precision.HIGHEST)
        return (total, None)

    stacked = (
        coarse.reshape(turns, block, coarse_rows, coarse.shape[2]),
        details.reshape(turns, block, 2),
    )
    start = jnp.zeros((tile_count, fine_rows, 2 * BY, 2 * BZ), jnp.float32)
    total, unused = lax.scan(one_block, start, stacked)
    return total


def shards(tables, weights, aperture):
    bricks = tables[0]
    own_weight = weights[0]
    own_mask = aperture[0]
    owners = lax.axis_size("tile")
    group = bricks.shape[0] // owners
    capacity = group // 2
    plane = bricks.shape[2]
    live = own_mask.reshape(owners, group)
    ranking = jnp.cumsum(live, axis=1) - 1
    slot_ids = jnp.arange(capacity)
    chosen = ((live[:, None, :] == 1) & (ranking[:, None, :] == slot_ids[None, :, None])).astype(
        jnp.int32
    )
    local_tile = jnp.sum(chosen * jnp.arange(group)[None, None, :], axis=2)
    occupied = jnp.sum(chosen, axis=2)
    brick_index = local_tile + jnp.arange(owners)[:, None] * group
    picked = bricks[brick_index]
    factor = own_weight[brick_index] * occupied.astype(jnp.float32)
    details = jnp.stack([factor, local_tile.astype(jnp.float32)], axis=-1)
    arrived, info = (
        lax.all_to_all(picked, "tile", split_axis=0, concat_axis=0, tiled=True),
        lax.all_to_all(details, "tile", split_axis=0, concat_axis=0, tiled=True),
    )
    partial_image = refine_accumulate(
        arrived.reshape(-1, BX, plane), info.reshape(-1, 2), 2 * BX, group
    )
    image = lax.psum_scatter(partial_image, "src", scatter_dimension=1, tiled=True)
    return image


def solution(mesh):
    placed = (
        P(("src", "tile"), None, None, None),
        P(("src", "tile"), None),
        P(("src", "tile"), None),
    )
    return jax.shard_map(
        shards, mesh=mesh, in_specs=placed, out_specs=P("tile", "src", None, None), check_vma=False
    )
```

profile of v0, /device:TPU:0, one launch (start us, length us, event | category | flops | bytes accessed | tf_op | source)
XLA Modules:
  0.0 567.6 jit_solution(8663999299811174132)
XLA Ops:
  10.6 5.2 all-to-all-start
  15.8 4.2 gather_fusion.1
  20.5 3.7 all-to-all-start.1
  24.2 26.6 %all-to-all-done.1 = f32[8,2,32,1024]{3,2,1,0:T(8,128)S(1)} async-done(((f32[8,2,32,1024]{3,2,1,0:T(8,128)}), f32[8,2,32,1024]{3,2,1,0:T(8,128)S(1)}, u32[]{:S(2)}, u32[]{:S(2)}) %all-to-all-start.1) | async-done | bytes 2097184 | tf_op jit(solution)/shard_map/all_to_all | solution.py:75
  50.8 424.1 %while.11 = (s32[]{:T(128)}, f32[4,64,32,128]{3,0,2,1:T(4,128)}, f32[8,2,2]{1,2,0:T(2,128)S(1)}, f32[8,2,32,1024]{3,2,1,0:T(8,128)S(1)}, s32[]{:T(128)}, /*index=5*/s32[]{:T(128)}) while((s32[]{:T(128)}, f32[4,64,32,128]{3,0,2,1:T(4,128)}, f32[8,2,2]{1,2,0:T(2,128)S(1)}, f32[8,2,32,1024]{3,2,1,0:T(8,128)S(1)}, s32[]{:T(128)}, ...), condition=%wide.region_4.5_spmd.clone, body=%wide.region_3.4_spmd.clone.sunk | while | flops 31916056 | bytes 108888480 | solution.py:50
  61.7 2.8 copy.171
  64.5 2.6 copy.172
  67.1 3.2 copy.173
  70.6 2.4 fusion.38
  73.0 3.7 copy.174
  80.7 6.7 %fusion.41 = f32[2,64,16,2,128]{4,2,3,1,0:T(8,128)S(1)} fusion(f32[2,64,16,1,128]{4,2,3,1,0:T(8,128)S(1)} %get-tuple-element.183, f32[2,64,16,1,128]{4,2,3,1,0:T(8,128)S(1)} %get-tuple-element.184), kind=kLoop, calls=%fused_computation.6.clone.1 | loop fusion | flops 1048576 | bytes 4194304 | tf_op jit(solution)/shard_map/while/body/eval_jaxpr/cos | solution.py:40
  89.6 12.2 %select_add_fusion.2 = f32[4,64,32,128]{3,0,2,1:T(4,128)S(1)} fusion(f32[4,64,32,128]{3,0,2,1:T(4,128)S(1)} %copy-done.2, f32[2,64,32,128]{3,1,2,0:T(8,128)S(1)} %bitcast.102, pred[]{:T(512)S(6)} %compare.3, f32[2]{0:T(128)S(1)} %get-tuple-element.185, f32[4]{0:T(128)S(1)} %iota_convert_fusion.2, f32[2]{0:T(128)S(1)} %get-tuple-element.186), kind=kOutput, calls=%fused_computation.3.clone.2 | convolution fusion | flops 27262992 | bytes 10485793 | tf_op jit(solution)/shard_map/while/body/eval_jaxpr/kp,kfyz->pfyz/dot_general | solution.py:42
  114.7 2.8 copy.171
  117.5 2.6 copy.172
  120.1 3.2 copy.173
  123.7 2.4 fusion.38
  126.1 3.7 copy.174
  133.7 6.7 %fusion.41 = f32[2,64,16,2,128]{4,2,3,1,0:T(8,128)S(1)} fusion(f32[2,64,16,1,128]{4,2,3,1,0:T(8,128)S(1)} %get-tuple-element.183, f32[2,64,16,1,128]{4,2,3,1,0:T(8,128)S(1)} %get-tuple-element.184), kind=kLoop, calls=%fused_computation.6.clone.1 | loop fusion | flops 1048576 | bytes 4194304 | tf_op jit(solution)/shard_map/while/body/eval_jaxpr/cos | solution.py:40
  142.7 12.2 %select_add_fusion.2 = f32[4,64,32,128]{3,0,2,1:T(4,128)S(1)} fusion(f32[4,64,32,128]{3,0,2,1:T(4,128)S(1)} %copy-done.2, f32[2,64,32,128]{3,1,2,0:T(8,128)S(1)} %bitcast.102, pred[]{:T(512)S(6)} %compare.3, f32[2]{0:T(128)S(1)} %get-tuple-element.185, f32[4]{0:T(128)S(1)} %iota_convert_fusion.2, f32[2]{0:T(128)S(1)} %get-tuple-element.186), kind=kOutput, calls=%fused_computation.3.clone.2 | convolution fusion | flops 27262992 | bytes 10485793 | tf_op jit(solution)/shard_map/while/body/eval_jaxpr/kp,kfyz->pfyz/dot_general | solution.py:42
  167.8 2.8 copy.171
  170.6 2.6 copy.172
  173.1 3.2 copy.173
  176.7 2.4 fusion.38
  179.1 3.7 copy.174
  186.7 6.7 %fusion.41 = f32[2,64,16,2,128]{4,2,3,1,0:T(8,128)S(1)} fusion(f32[2,64,16,1,128]{4,2,3,1,0:T(8,128)S(1)} %get-tuple-element.183, f32[2,64,16,1,128]{4,2,3,1,0:T(8,128)S(1)} %get-tuple-element.184), kind=kLoop, calls=%fused_computation.6.clone.1 | loop fusion | flops 1048576 | bytes 4194304 | tf_op jit(solution)/shard_map/while/body/eval_jaxpr/cos | solution.py:40
  195.7 12.2 %select_add_fusion.2 = f32[4,64,32,128]{3,0,2,1:T(4,128)S(1)} fusion(f32[4,64,32,128]{3,0,2,1:T(4,128)S(1)} %copy-done.2, f32[2,64,32,128]{3,1,2,0:T(8,128)S(1)} %bitcast.102, pred[]{:T(512)S(6)} %compare.3, f32[2]{0:T(128)S(1)} %get-tuple-element.185, f32[4]{0:T(128)S(1)} %iota_convert_fusion.2, f32[2]{0:T(128)S(1)} %get-tuple-element.186), kind=kOutput, calls=%fused_computation.3.clone.2 | convolution fusion | flops 27262992 | bytes 10485793 | tf_op jit(solution)/shard_map/while/body/eval_jaxpr/kp,kfyz->pfyz/dot_general | solution.py:42
  220.8 2.8 copy.171
  223.6 2.6 copy.172
  226.2 3.2 copy.173
  229.7 2.4 fusion.38
  232.1 3.7 copy.174
  239.8 6.7 %fusion.41 = f32[2,64,16,2,128]{4,2,3,1,0:T(8,128)S(1)} fusion(f32[2,64,16,1,128]{4,2,3,1,0:T(8,128)S(1)} %get-tuple-element.183, f32[2,64,16,1,128]{4,2,3,1,0:T(8,128)S(1)} %get-tuple-element.184), kind=kLoop, calls=%fused_computation.6.clone.1 | loop fusion | flops 1048576 | bytes 4194304 | tf_op jit(solution)/shard_map/while/body/eval_jaxpr/cos | solution.py:40
  248.7 12.2 %select_add_fusion.2 = f32[4,64,32,128]{3,0,2,1:T(4,128)S(1)} fusion(f32[4,64,32,128]{3,0,2,1:T(4,128)S(1)} %copy-done.2, f32[2,64,32,128]{3,1,2,0:T(8,128)S(1)} %bitcast.102, pred[]{:T(512)S(6)} %compare.3, f32[2]{0:T(128)S(1)} %get-tuple-element.185, f32[4]{0:T(128)S(1)} %iota_convert_fusion.2, f32[2]{0:T(128)S(1)} %get-tuple-element.186), kind=kOutput, calls=%fused_computation.3.clone.2 | convolution fusion | flops 27262992 | bytes 10485793 | tf_op jit(solution)/shard_map/while/body/eval_jaxpr/kp,kfyz->pfyz/dot_general | solution.py:42
  273.8 2.8 copy.171
  276.6 2.6 copy.172
  279.2 3.2 copy.173
  282.7 2.4 fusion.38
  285.1 3.7 copy.174
  292.8 6.7 %fusion.41 = f32[2,64,16,2,128]{4,2,3,1,0:T(8,128)S(1)} fusion(f32[2,64,16,1,128]{4,2,3,1,0:T(8,128)S(1)} %get-tuple-element.183, f32[2,64,16,1,128]{4,2,3,1,0:T(8,128)S(1)} %get-tuple-element.184), kind=kLoop, calls=%fused_computation.6.clone.1 | loop fusion | flops 1048576 | bytes 4194304 | tf_op jit(solution)/shard_map/while/body/eval_jaxpr/cos | solution.py:40
  301.7 12.2 %select_add_fusion.2 = f32[4,64,32,128]{3,0,2,1:T(4,128)S(1)} fusion(f32[4,64,32,128]{3,0,2,1:T(4,128)S(1)} %copy-done.2, f32[2,64,32,128]{3,1,2,0:T(8,128)S(1)} %bitcast.102, pred[]{:T(512)S(6)} %compare.3, f32[2]{0:T(128)S(1)} %get-tuple-element.185, f32[4]{0:T(128)S(1)} %iota_convert_fusion.2, f32[2]{0:T(128)S(1)} %get-tuple-element.186), kind=kOutput, calls=%fused_computation.3.clone.2 | convolution fusion | flops 27262992 | bytes 10485793 | tf_op jit(solution)/shard_map/while/body/eval_jaxpr/kp,kfyz->pfyz/dot_general | solution.py:42
  326.8 2.8 copy.171
  329.6 2.6 copy.172
  332.2 3.2 copy.173
  335.7 2.4 fusion.38
  338.1 3.7 copy.174
  345.8 6.7 %fusion.41 = f32[2,64,16,2,128]{4,2,3,1,0:T(8,128)S(1)} fusion(f32[2,64,16,1,128]{4,2,3,1,0:T(8,128)S(1)} %get-tuple-element.183, f32[2,64,16,1,128]{4,2,3,1,0:T(8,128)S(1)} %get-tuple-element.184), kind=kLoop, calls=%fused_computation.6.clone.1 | loop fusion | flops 1048576 | bytes 4194304 | tf_op jit(solution)/shard_map/while/body/eval_jaxpr/cos | solution.py:40
  354.7 12.2 %select_add_fusion.2 = f32[4,64,32,128]{3,0,2,1:T(4,128)S(1)} fusion(f32[4,64,32,128]{3,0,2,1:T(4,128)S(1)} %copy-done.2, f32[2,64,32,128]{3,1,2,0:T(8,128)S(1)} %bitcast.102, pred[]{:T(512)S(6)} %compare.3, f32[2]{0:T(128)S(1)} %get-tuple-element.185, f32[4]{0:T(128)S(1)} %iota_convert_fusion.2, f32[2]{0:T(128)S(1)} %get-tuple-element.186), kind=kOutput, calls=%fused_computation.3.clone.2 | convolution fusion | flops 27262992 | bytes 10485793 | tf_op jit(solution)/shard_map/while/body/eval_jaxpr/kp,kfyz->pfyz/dot_general | solution.py:42
  379.8 2.8 copy.171
  382.6 2.6 copy.172
  385.2 3.2 copy.173
  388.8 2.4 fusion.38
  391.1 3.7 copy.174
  398.8 6.7 %fusion.41 = f32[2,64,16,2,128]{4,2,3,1,0:T(8,128)S(1)} fusion(f32[2,64,16,1,128]{4,2,3,1,0:T(8,128)S(1)} %get-tuple-element.183, f32[2,64,16,1,128]{4,2,3,1,0:T(8,128)S(1)} %get-tuple-element.184), kind=kLoop, calls=%fused_computation.6.clone.1 | loop fusion | flops 1048576 | bytes 4194304 | tf_op jit(solution)/shard_map/while/body/eval_jaxpr/cos | solution.py:40
  407.8 12.2 %select_add_fusion.2 = f32[4,64,32,128]{3,0,2,1:T(4,128)S(1)} fusion(f32[4,64,32,128]{3,0,2,1:T(4,128)S(1)} %copy-done.2, f32[2,64,32,128]{3,1,2,0:T(8,128)S(1)} %bitcast.102, pred[]{:T(512)S(6)} %compare.3, f32[2]{0:T(128)S(1)} %get-tuple-element.185, f32[4]{0:T(128)S(1)} %iota_convert_fusion.2, f32[2]{0:T(128)S(1)} %get-tuple-element.186), kind=kOutput, calls=%fused_computation.3.clone.2 | convolution fusion | flops 27262992 | bytes 10485793 | tf_op jit(solution)/shard_map/while/body/eval_jaxpr/kp,kfyz->pfyz/dot_general | solution.py:42
  432.8 2.8 copy.171
  435.7 2.6 copy.172
  438.2 3.2 copy.173
  441.8 2.4 fusion.38
  444.2 3.7 copy.174
  451.8 6.7 %fusion.41 = f32[2,64,16,2,128]{4,2,3,1,0:T(8,128)S(1)} fusion(f32[2,64,16,1,128]{4,2,3,1,0:T(8,128)S(1)} %get-tuple-element.183, f32[2,64,16,1,128]{4,2,3,1,0:T(8,128)S(1)} %get-tuple-element.184), kind=kLoop, calls=%fused_computation.6.clone.1 | loop fusion | flops 1048576 | bytes 4194304 | tf_op jit(solution)/shard_map/while/body/eval_jaxpr/cos | solution.py:40
  460.8 12.2 %select_add_fusion.2 = f32[4,64,32,128]{3,0,2,1:T(4,128)S(1)} fusion(f32[4,64,32,128]{3,0,2,1:T(4,128)S(1)} %copy-done.2, f32[2,64,32,128]{3,1,2,0:T(8,128)S(1)} %bitcast.102, pred[]{:T(512)S(6)} %compare.3, f32[2]{0:T(128)S(1)} %get-tuple-element.185, f32[4]{0:T(128)S(1)} %iota_convert_fusion.2, f32[2]{0:T(128)S(1)} %get-tuple-element.186), kind=kOutput, calls=%fused_computation.3.clone.2 | convolution fusion | flops 27262992 | bytes 10485793 | tf_op jit(solution)/shard_map/while/body/eval_jaxpr/kp,kfyz->pfyz/dot_general | solution.py:42
  474.9 2.7 copy.132
  477.6 4.3 copy.147
  482.0 76.3 %reduce-scatter.5.cloned.1.call-done = f32[16,16384]{1,0:T(8,128)} async-done(((f32[64,16384]{1,0:T(8,128)}), f32[16,16384]{1,0:T(8,128)}) %reduce-scatter.5.cloned.1.call-update) | async-done | bytes 1048592
  (341 shorter events, 161.6 us)
Async XLA Ops:
  6.5 2.5 copy-start
  10.6 9.9 %all-to-all-start = ((f32[8,2,2]{1,2,0:T(2,128)}), f32[8,2,2]{1,2,0:T(2,128)S(1)}, u32[]{:S(2)}, u32[]{:S(2)}) async-start(f32[8,2,2]{1,2,0:T(2,128)} %copy.127), calls=%async_computation | async-start | bytes 16384 | tf_op jit(solution)/shard_map/all_to_all | solution.py:76
  20.5 30.3 %all-to-all-start.1 = ((f32[8,2,32,1024]{3,2,1,0:T(8,128)}), f32[8,2,32,1024]{3,2,1,0:T(8,128)S(1)}, u32[]{:S(2)}, u32[]{:S(2)}) async-start(f32[8,2,32,1024]{3,2,1,0:T(8,128)} %bitcast.4), calls=%async_computation.1 | async-start | bytes 4194304 | tf_op jit(solution)/shard_map/all_to_all | solution.py:75
  24.2 534.2 %reduce-scatter.5.cloned.1.call-start = ((), (), s32[]{:S(2)}) async-start(), calls=%async_computation.3 | async-start | bytes 5242880
  50.8 1.3 copy-start.5
  58.2 1.2 copy-start.4
  73.0 3.7 copy-start.1
  87.5 2.2 copy-start.2
  89.6 14.1 %copy-start.6 = (f32[8,2,32,1024]{3,2,1,0:T(8,128)S(1)}, f32[8,2,32,1024]{3,2,1,0:T(8,128)}, u32[]{:S(2)}) copy-start(f32[8,2,32,1024]{3,2,1,0:T(8,128)} %copy-done.5) | copy-start | bytes 6291460 | tf_op jit(solution)/shard_map/while
  101.9 1.9 copy-start.3
  103.8 1.3 copy-start.5
  111.2 1.2 copy-start.4
  126.1 3.7 copy-start.1
  140.5 2.2 copy-start.2
  142.7 14.1 %copy-start.6 = (f32[8,2,32,1024]{3,2,1,0:T(8,128)S(1)}, f32[8,2,32,1024]{3,2,1,0:T(8,128)}, u32[]{:S(2)}) copy-start(f32[8,2,32,1024]{3,2,1,0:T(8,128)} %copy-done.5) | copy-start | bytes 6291460 | tf_op jit(solution)/shard_map/while
  154.9 1.9 copy-start.3
  156.8 1.3 copy-start.5
  164.2 1.2 copy-start.4
  179.1 3.7 copy-start.1
  193.5 2.2 copy-start.2
  195.7 14.1 %copy-start.6 = (f32[8,2,32,1024]{3,2,1,0:T(8,128)S(1)}, f32[8,2,32,1024]{3,2,1,0:T(8,128)}, u32[]{:S(2)}) copy-start(f32[8,2,32,1024]{3,2,1,0:T(8,128)} %copy-done.5) | copy-start | bytes 6291460 | tf_op jit(solution)/shard_map/while
  207.9 1.9 copy-start.3
  209.8 1.3 copy-start.5
  217.2 1.2 copy-start.4
  232.1 3.7 copy-start.1
  246.5 2.2 copy-start.2
  248.7 14.1 %copy-start.6 = (f32[8,2,32,1024]{3,2,1,0:T(8,128)S(1)}, f32[8,2,32,1024]{3,2,1,0:T(8,128)}, u32[]{:S(2)}) copy-start(f32[8,2,32,1024]{3,2,1,0:T(8,128)} %copy-done.5) | copy-start | bytes 6291460 | tf_op jit(solution)/shard_map/while
  260.9 1.9 copy-start.3
  262.8 1.3 copy-start.5
  270.2 1.2 copy-start.4
  285.1 3.7 copy-start.1
  299.5 2.2 copy-start.2
  301.7 14.1 %copy-start.6 = (f32[8,2,32,1024]{3,2,1,0:T(8,128)S(1)}, f32[8,2,32,1024]{3,2,1,0:T(8,128)}, u32[]{:S(2)}) copy-start(f32[8,2,32,1024]{3,2,1,0:T(8,128)} %copy-done.5) | copy-start | bytes 6291460 | tf_op jit(solution)/shard_map/while
  313.9 1.9 copy-start.3
  315.9 1.3 copy-start.5
  323.2 1.2 copy-start.4
  338.1 3.7 copy-start.1
  352.5 2.2 copy-start.2
  354.7 14.1 %copy-start.6 = (f32[8,2,32,1024]{3,2,1,0:T(8,128)S(1)}, f32[8,2,32,1024]{3,2,1,0:T(8,128)}, u32[]{:S(2)}) copy-start(f32[8,2,32,1024]{3,2,1,0:T(8,128)} %copy-done.5) | copy-start | bytes 6291460 | tf_op jit(solution)/shard_map/while
  366.9 1.9 copy-start.3
  368.9 1.3 copy-start.5
  376.3 1.2 copy-start.4
  391.1 3.7 copy-start.1
  405.6 2.2 copy-start.2
  407.8 14.1 %copy-start.6 = (f32[8,2,32,1024]{3,2,1,0:T(8,128)S(1)}, f32[8,2,32,1024]{3,2,1,0:T(8,128)}, u32[]{:S(2)}) copy-start(f32[8,2,32,1024]{3,2,1,0:T(8,128)} %copy-done.5) | copy-start | bytes 6291460 | tf_op jit(solution)/shard_map/while
  420.0 1.9 copy-start.3
  421.9 1.3 copy-start.5
  429.3 1.2 copy-start.4
  444.2 3.7 copy-start.1
  458.6 2.2 copy-start.2
  460.8 14.1 %copy-start.6 = (f32[8,2,32,1024]{3,2,1,0:T(8,128)S(1)}, f32[8,2,32,1024]{3,2,1,0:T(8,128)}, u32[]{:S(2)}) copy-start(f32[8,2,32,1024]{3,2,1,0:T(8,128)} %copy-done.5) | copy-start | bytes 6291460 | tf_op jit(solution)/shard_map/while
  473.0 1.9 copy-start.3
Sparse Core Ops, SparseCore 0:
  482.1 76.1 reduce-scatter.4
where the time goes:
time: 570 us; the launch traced here: 568 us
  local copies, waits for them, and re-layouts  250 us (44%)
  waiting for transfers between devices  103 us (18%)
  matrix products  97.6 us (17%)
  other arithmetic  92.7 us (16%)
  between operations  13.5 us (2%)
  starting transfers between devices  8.92 us (2%)
    dot_general x8, matrix products, one_block(): jnp.einsum('kp,kfyz->pfyz', select, phase, precision=lax.Precision.HIGHEST)  97.6 us
    while x128, local copies, waits for them, and re-layouts  82 us
    unnamed x2, waiting for transfers between devices  76.4 us
    cos x8, other arithmetic, one_block(): phase = jnp.cos(angular_rate * fine)  54 us
    mul x32, local copies, waits for them, and re-layouts, refine_axis(): even_rows = 0.75 * values + 0.25 * lower  45.3 us
    all_to_all x1, waiting for transfers between devices, shards(): lax.all_to_all(picked, 'tile', split_axis=0, concat_axis=0, tiled=True)  26.6 us
    another operation x16, local copies, waits for them, and re-layouts, refine_axis(): paired = jnp.stack([even_rows, odd_rows], axis=axis + 1)  26.5 us
    slice x24, local copies, waits for them, and re-layouts, refine_axis(): first = lax.slice_in_dim(values, 0, 1, axis=axis)  25.2 us
  transfers between devices with their start and end apart: 3, of which 3 were waited for; matrix products, arithmetic and copies ran while one was open for 1% of the time, Pallas kernels for 0%

commit v1 on v0

--- a/solution.py
+++ b/solution.py
@@ -1,12 +1,19 @@
+import functools
+import math
+
 import jax
 import jax.numpy as jnp
+import numpy as np
 from jax import lax
+from jax.experimental import pallas as pl
+from jax.experimental.pallas import tpu as pltpu
 from jax.sharding import PartitionSpec as P
 
 BX = 32
 BY = 16
 BZ = 64
-
+SUB = 8
+LANES = 128
 
 angular_rate = 9.0
 
@@ -51,7 +58,7 @@
     return total
 
 
-def shards(tables, weights, aperture):
+def general_shards(tables, weights, aperture):
     bricks = tables[0]
     own_weight = weights[0]
     own_mask = aperture[0]
@@ -78,8 +85,227 @@
     partial_image = refine_accumulate(
         arrived.reshape(-1, BX, plane), info.reshape(-1, 2), 2 * BX, group
     )
-    image = lax.psum_scatter(partial_image, "src", scatter_dimension=1, tiled=True)
-    return image
+    return lax.psum_scatter(partial_image, "src", scatter_dimension=1, tiled=True)
+
+
+YP = BY * BZ // LANES
+HALO_LO = YP
+HALO_HI = YP + 1
+BLOCK = YP + 2
+
+
+def cos_series():
+    nodes = 400
+    v = 0.125 + 0.125 * np.cos(np.pi * (np.arange(nodes) + 0.5) / nodes)
+    cheb = np.polynomial.chebyshev.Chebyshev.fit(
+        v, np.cos(2 * np.pi * np.sqrt(v)), 5, domain=[0.0, 0.25]
+    )
+    return [float(c) for c in cheb.convert(kind=np.polynomial.Polynomial, domain=[-1, 1]).coef]
+
+
+def refine_columns():
+    m = np.zeros((2 * BZ, BZ), np.float64)
+    for i in range(2 * BZ):
+        k = i // 2
+        other = max(k - 1, 0) if i % 2 == 0 else min(k + 1, BZ - 1)
+        m[i, k] += 0.75
+        m[i, other] += 0.25
+    out = np.zeros((2, 2, BZ, 2, 2, 2 * BZ), np.float64)
+    for split in range(2):
+        for scale, factor in enumerate((0.75, 0.25)):
+            for parity in range(2):
+                out[split, parity, :, scale, parity, :] = factor * m.T
+    return out.reshape(4 * BZ, 8 * BZ)
+
+
+def slot_scalars(mask_ref, weight_ref, first, group, slot):
+    count = jnp.int32(0)
+    local = jnp.int32(0)
+    weight = jnp.float32(0.0)
+    for i in range(group):
+        live = mask_ref[0, first + i] == 1
+        hit = jnp.logical_and(live, count == slot)
+        local = jnp.where(hit, jnp.int32(i), local)
+        weight = jnp.where(hit, weight_ref[0, first + i], weight)
+        count = count + live.astype(jnp.int32)
+    return local, weight
+
+
+def put_halo(out_ref, where, row):
+    for y in range(YP):
+        out_ref[where + (pl.ds(y, 1), slice(None))] = row[:, y * LANES : (y + 1) * LANES]
+
+
+def pick_kernel(quarters, owners, group, capacity, mask_ref, weight_ref, tables_ref, out_ref, buf, sem):
+    def copy(g, j):
+        local, _ = slot_scalars(mask_ref, weight_ref, g * group, group, j)
+        return pltpu.make_async_copy(
+            tables_ref.at[g * group + local], buf.at[g * capacity + j], sem.at[g * capacity + j]
+        )
+
+    for g in range(owners):
+        for j in range(capacity):
+            copy(g, j).start()
+    rows = lax.broadcasted_iota(jnp.int32, (SUB, LANES), 0)
+    lanes = lax.broadcasted_iota(jnp.int32, (SUB, LANES), 1)
+    for g in range(owners):
+        info = jnp.zeros((SUB, LANES), jnp.float32)
+        for j in range(capacity):
+            local, weight = slot_scalars(mask_ref, weight_ref, g * group, group, j)
+            info = jnp.where(lanes == 2 * j, weight, info)
+            info = jnp.where(lanes == 2 * j + 1, local.astype(jnp.float32), info)
+        for q in range(quarters):
+            out_ref[q * owners + g, capacity * BLOCK] = info
+        for j in range(capacity):
+            s = g * capacity + j
+            copy(g, j).wait()
+            for q in range(quarters):
+                d = q * owners + g
+                for y in range(YP):
+                    out_ref[d, j * BLOCK + y] = buf[s, q, :, y * LANES : (y + 1) * LANES]
+                lo = buf[s, q - 1, 7:8, :] if q > 0 else buf[s, 0, 0:1, :]
+                hi = buf[s, q + 1, 0:1, :] if q < quarters - 1 else buf[s, q, 7:8, :]
+                put_halo(out_ref, (d, j * BLOCK + HALO_LO), lo)
+                put_halo(out_ref, (d, j * BLOCK + HALO_HI), hi)
+
+
+def pick(tables, weights, aperture, quarters, owners, group, capacity):
+    n = quarters * owners
+    blocks = capacity * BLOCK + 1
+    return pl.pallas_call(
+        functools.partial(pick_kernel, quarters, owners, group, capacity),
+        name="pick",
+        out_shape=jax.ShapeDtypeStruct((n, blocks, SUB, LANES), jnp.float32),
+        in_specs=[
+            pl.BlockSpec(memory_space=pltpu.SMEM),
+            pl.BlockSpec(memory_space=pltpu.SMEM),
+            pl.BlockSpec(memory_space=pl.ANY),
+        ],
+        out_specs=pl.BlockSpec(memory_space=pltpu.VMEM),
+        scratch_shapes=[
+            pltpu.VMEM((owners * capacity, quarters, SUB, YP * LANES), jnp.float32),
+            pltpu.SemaphoreType.DMA((owners * capacity,)),
+        ],
+    )(aperture, weights, tables.reshape(-1, quarters, SUB, YP * LANES))
+
+
+def add_slot(acc_ref, series, block, low, high, columns, weight, tile):
+    rows = lax.broadcasted_iota(jnp.int32, (SUB, LANES), 0)
+    turns = angular_rate / (2 * math.pi)
+    near, away = 0.75 * turns, 0.25 * turns
+    even, odd = [], []
+    for y in range(YP):
+        c = block(y)
+        down = jnp.where(rows == 0, jnp.broadcast_to(low(y), c.shape), pltpu.roll(c, 1, 0))
+        up = jnp.where(rows == SUB - 1, jnp.broadcast_to(high(y), c.shape), pltpu.roll(c, SUB - 1, 0))
+        mid = near * c
+        even.append(mid + away * down)
+        odd.append(mid + away * up)
+    x = jnp.concatenate(even + odd, axis=0)
+    top = x.astype(jnp.bfloat16)
+    rest = (x - top.astype(jnp.float32)).astype(jnp.bfloat16)
+    res = jnp.dot(jnp.concatenate([top, rest], axis=1), columns, preferred_element_type=jnp.float32)
+    scaled = [weight * c for c in series]
+
+    def part(parity, y, k):
+        r = (parity * YP + y) * SUB
+        return res[r : r + SUB, k * LANES : (k + 1) * LANES]
+
+    for parity in range(2):
+        for y in range(YP):
+            te, to, he, ho = (part(parity, y, k) for k in range(4))
+            before = part(parity, y - 1, 3) if y > 0 else he
+            after = part(parity, y + 1, 2) if y < YP - 1 else ho
+            for k, t in enumerate((te + before, te + ho, to + he, to + after)):
+                r = t - jnp.round(t)
+                u = r * r
+                p = scaled[5]
+                for c in scaled[4:0:-1]:
+                    p = p * u + c
+                where = (tile, parity, 4 * y + k)
+                acc_ref[where] = acc_ref[where] + p * u
+
+
+def image_kernel(step, capacity, series, tiles, in_ref, all_ref, columns_ref, out_ref, acc, info, bias, sem):
+    i = pl.program_id(0)
+    copy = pltpu.make_async_copy(all_ref.at[:, capacity * BLOCK, pl.ds(0, 1), :], info, sem)
+
+    @pl.when(i == 0)
+    def _():
+        copy.start()
+        acc[...] = jnp.zeros_like(acc)
+        for t in range(tiles):
+            bias[t] = jnp.float32(0.0)
+        copy.wait()
+
+    columns = columns_ref[...]
+
+    def one(n, carry):
+        for j in range(capacity):
+            weight = info[i * step + n, 0, 2 * j]
+            tile = info[i * step + n, 0, 2 * j + 1].astype(jnp.int32)
+            bias[tile] = bias[tile] + weight * series[0]
+            add_slot(
+                acc,
+                series,
+                lambda y: in_ref[n, j * BLOCK + y],
+                lambda y: in_ref[n, j * BLOCK + HALO_LO, pl.ds(y, 1), :],
+                lambda y: in_ref[n, j * BLOCK + HALO_HI, pl.ds(y, 1), :],
+                columns,
+                weight,
+                tile,
+            )
+        return carry
+
+    lax.fori_loop(0, step, one, 0)
+
+    @pl.when(i == pl.num_programs(0) - 1)
+    def _():
+        span = 2 * SUB * 2 * BY
+
+        def flush(t, carry):
+            for parity in range(2):
+                for y in range(2 * BY):
+                    start = t * span + parity * 2 * BY + y
+                    out_ref[pl.ds(start, SUB, stride=4 * BY), :] = acc[t, parity, y] + bias[t]
+            return carry
+
+        lax.fori_loop(0, tiles, flush, 0)
+
+
+def image_of(arrived, tiles, capacity):
+    n, blocks = arrived.shape[:2]
+    step = 4
+    columns = jnp.asarray(refine_columns(), jnp.bfloat16)
+    rows = tiles * 2 * SUB * 2 * BY
+    return pl.pallas_call(
+        functools.partial(image_kernel, step, capacity, cos_series(), tiles),
+        name="image",
+        grid=(n // step,),
+        out_shape=jax.ShapeDtypeStruct((rows, LANES), jnp.float32),
+        in_specs=[
+            pl.BlockSpec((step, blocks, SUB, LANES), lambda i: (i, 0, 0, 0)),
+            pl.BlockSpec(memory_space=pl.ANY),
+            pl.BlockSpec(columns.shape, lambda i: (0, 0)),
+        ],
+        out_specs=pl.BlockSpec((rows, LANES), lambda i: (0, 0)),
+        scratch_shapes=[
+            pltpu.VMEM((tiles, 2, 2 * BY, SUB, LANES), jnp.float32),
+            pltpu.SMEM((n, 1, LANES), jnp.float32),
+            pltpu.SMEM((tiles,), jnp.float32),
+            pltpu.SemaphoreType.DMA,
+        ],
+    )(arrived, arrived, columns)
+
+
+def octet_shards(tables, weights, aperture):
+    quarters, owners = lax.axis_size("src"), lax.axis_size("tile")
+    group = tables.shape[1] // owners
+    capacity = group // 2
+    sent = pick(tables[0], weights, aperture, quarters, owners, group, capacity)
+    arrived = lax.all_to_all(sent, ("src", "tile"), split_axis=0, concat_axis=0, tiled=True)
+    image = image_of(arrived, group, capacity)
+    return image.reshape(group, 2 * SUB, 2 * BY, 2 * BZ)
 
 
 def solution(mesh):
@@ -88,6 +314,11 @@
         P(("src", "tile"), None),
         P(("src", "tile"), None),
     )
+    fits = BX == mesh.shape["src"] * SUB
     return jax.shard_map(
-        shards, mesh=mesh, in_specs=placed, out_specs=P("tile", "src", None, None), check_vma=False
-    )
+        octet_shards if fits else general_shards,
+        mesh=mesh,
+        in_specs=placed,
+        out_specs=P("tile", "src", None, None),
+        check_vma=False,
+    )

time: 570 us -> 91.9 us (0.16)
  local copies, waits for them, and re-layouts: 250 us -> 0 us
  waiting for transfers between devices: 103 us -> 0 us
  matrix products: 97.6 us -> 0 us
  other arithmetic: 92.7 us -> 0 us
  blocking collectives: 0 us -> 70.4 us
  Pallas kernels: 0 us -> 21.1 us
  between operations: 13.5 us -> 0.01 us
  starting transfers between devices: 8.92 us -> 0 us
    dot_general x8 -> x0, matrix products: 97.6 us -> none  [one_block(): jnp.einsum('kp,kfyz->pfyz', select, phase, precision=lax.Precision.HIGHEST)]
    while x128 -> x0, local copies, waits for them, and re-layouts: 82 us -> none
    unnamed x2 -> x0, waiting for transfers between devices: 76.4 us -> none
    all_to_all x0 -> x1, blocking collectives: none -> 70.4 us  [octet_shards(): lax.all_to_all(sent, ('src', 'tile'), split_axis=0, concat_axis=0, tiled=...]
    cos x8 -> x0, other arithmetic: 54 us -> none  [one_block(): phase = jnp.cos(angular_rate * fine)]
    slice x48 -> x0, local copies, waits for them, and re-layouts: 49.6 us -> none  [the longest x24 25.2 us: refine_axis(): first = lax.slice_in_dim(values, 0, 1, axis=axis)]
    mul x32 -> x0, local copies, waits for them, and re-layouts: 45.3 us -> none  [refine_axis(): even_rows = 0.75 * values + 0.25 * lower]
    another operation x18 -> x0, local copies, waits for them, and re-layouts: 27.3 us -> none  [the longest x16 26.5 us: refine_axis(): paired = jnp.stack([even_rows, odd_rows], axis=axis + 1)]
  transfers between devices with their start and end apart: 3 -> 0, of which waited for: 3 -> 0; matrix products, arithmetic and copies ran while one was open for 1% -> 0% of each run, Pallas kernels for 0% -> 0%
where the time goes in v1:
time: 91.9 us; the launch traced here: 91.5 us
  blocking collectives  70.4 us (77%)
  Pallas kernels  21.1 us (23%)
    all_to_all x1, blocking collectives, octet_shards(): lax.all_to_all(sent, ('src', 'tile'), split_axis=0, concat_axis=0, tiled=...  70.4 us
    pallas_call x1, Pallas kernels, image_of(): pl.pallas_call(functools.partial(image_kernel, step, capacity, cos_series...  17.1 us
    pallas_call x1, Pallas kernels, pick(): pl.pallas_call(functools.partial(pick_kernel, quarters, owners, group, ca...  4.04 us

profile of v1, /device:TPU:0, one launch (start us, length us, event | category | flops | bytes accessed | tf_op | source)
XLA Modules:
  0.0 91.5 jit_solution(298129542106328557)
XLA Ops:
  0.0 4.0 %pick.1 = f32[32,21,8,128]{3,2,1,0:T(8,128)} custom-call(s32[1,32]{1,0:T(1,128)} %mask_ref.1, f32[1,32]{1,0:T(1,128)} %weight_ref.1, f32[32,4,8,1024]{3,2,1,0:T(8,128)} %bitcast.2), custom_call_target="tpu_custom_call" | custom-call | tf_op jit(solution)/shard_map/pick/pallas_call | solution.py:175
  4.1 70.4 %all_to_all.5.in_ref.all_ref = f32[32,21,8,128]{3,2,1,0:T(8,128)} all-to-all(f32[32,21,8,128]{3,2,1,0:T(8,128)} %pick.1), channel_id=1, replica_groups=mesh['src'=4,'tile'=8] {'src','tile'}, dimensions={0} | all-to-all | bytes 5505024 | tf_op jit(solution)/shard_map/all_to_all | solution.py:306
  74.4 17.1 %image.1 = f32[2048,128]{1,0:T(8,128)} custom-call(f32[32,21,8,128]{3,2,1,0:T(8,128)} %all_to_all.5.in_ref.all_ref, f32[32,21,8,128]{3,2,1,0:T(8,128)} %all_to_all.5.in_ref.all_ref, bf16[256,512]{1,0:T(8,128)(2,1)} %constant.2.clone.columns_ref), custom_call_target="tpu_custom_call" | custom-call | tf_op jit(solution)/shard_map/image/pallas_call | solution.py:281

commit v2 on v0

--- a/solution.py
+++ b/solution.py
@@ -1,12 +1,20 @@
+import functools
+import math
+
 import jax
 import jax.numpy as jnp
+import numpy as np
 from jax import lax
+from jax.experimental import pallas as pl
+from jax.experimental.pallas import tpu as pltpu
 from jax.sharding import PartitionSpec as P
+
 
 BX = 32
 BY = 16
 BZ = 64
-
+SUB = 8
+LANES = 128
 
 angular_rate = 9.0
 
@@ -47,11 +55,11 @@
         details.reshape(turns, block, 2),
     )
     start = jnp.zeros((tile_count, fine_rows, 2 * BY, 2 * BZ), jnp.float32)
-    total, unused = lax.scan(one_block, start, stacked)
+    total, _ = lax.scan(one_block, start, stacked)
     return total
 
 
-def shards(tables, weights, aperture):
+def general_shards(tables, weights, aperture):
     bricks = tables[0]
     own_weight = weights[0]
     own_mask = aperture[0]
@@ -78,8 +86,313 @@
     partial_image = refine_accumulate(
         arrived.reshape(-1, BX, plane), info.reshape(-1, 2), 2 * BX, group
     )
-    image = lax.psum_scatter(partial_image, "src", scatter_dimension=1, tiled=True)
-    return image
+    return lax.psum_scatter(partial_image, "src", scatter_dimension=1, tiled=True)
+
+
+YP = BY * BZ // LANES
+BLOCK = YP + 2
+SLOTS = 2
+SIDE = SLOTS * BLOCK
+MESSAGE = 2 * SIDE + 1
+FINE = 2 * BY
+
+
+def cos_series():
+    nodes = 400
+    v = 0.125 + 0.125 * np.cos(np.pi * (np.arange(nodes) + 0.5) / nodes)
+    cheb = np.polynomial.chebyshev.Chebyshev.fit(
+        v, np.cos(2 * np.pi * np.sqrt(v)), 5, domain=[0.0, 0.25]
+    )
+    return [float(c) for c in cheb.convert(kind=np.polynomial.Polynomial, domain=[-1, 1]).coef]
+
+
+def refine_columns():
+    m = np.zeros((2 * BZ, BZ), np.float64)
+    for i in range(2 * BZ):
+        k = i // 2
+        other = max(k - 1, 0) if i % 2 == 0 else min(k + 1, BZ - 1)
+        m[i, k] += 0.75
+        m[i, other] += 0.25
+    out = np.zeros((2, 2, BZ, 2, 2, 2 * BZ), np.float64)
+    for split in range(2):
+        for scale, factor in enumerate((0.75, 0.25)):
+            for parity in range(2):
+                out[split, parity, :, scale, parity, :] = factor * m.T
+    return out.reshape(4 * BZ, 8 * BZ)
+
+
+def slot_scalars(mask_ref, weight_ref, first, group, slot):
+    count = jnp.int32(0)
+    local = jnp.int32(0)
+    weight = jnp.float32(0.0)
+    for i in range(group):
+        live = mask_ref[0, first + i] == 1
+        hit = jnp.logical_and(live, count == slot)
+        local = jnp.where(hit, jnp.int32(i), local)
+        weight = jnp.where(hit, weight_ref[0, first + i], weight)
+        count = count + live.astype(jnp.int32)
+    return local, weight
+
+
+def pick_kernel(sends, quarters, owners, group, mask_ref, weight_ref, tables_ref, *refs):
+    outs, (buf, sem) = refs[: len(sends)], refs[len(sends) :]
+    copies = []
+    for g in range(owners):
+        for j in range(SLOTS):
+            local, _ = slot_scalars(mask_ref, weight_ref, g * group, group, j)
+            s = g * SLOTS + j
+            copy = pltpu.make_async_copy(tables_ref.at[g * group + local], buf.at[s], sem.at[s])
+            copy.start()
+            copies.append(copy)
+    r, t = lax.axis_index("src"), lax.axis_index("tile")
+    lanes = lax.broadcasted_iota(jnp.int32, (SUB, LANES), 1)
+    for out_ref, (dz, dt) in zip(outs, sends):
+        info = jnp.zeros((SUB, LANES), jnp.float32)
+        for side in range(2):
+            g = t ^ (dt ^ side)
+            for j in range(SLOTS):
+                local, weight = slot_scalars(mask_ref, weight_ref, g * group, group, j)
+                lane = 2 * (side * SLOTS + j)
+                info = jnp.where(lanes == lane, weight, info)
+                info = jnp.where(lanes == lane + 1, local.astype(jnp.float32), info)
+        out_ref[SIDE] = info
+    for copy in copies:
+        copy.wait()
+    for out_ref, (dz, dt) in zip(outs, sends):
+        q = r ^ dz
+        below, above = jnp.maximum(q - 1, 0), jnp.minimum(q + 1, quarters - 1)
+        for side in range(2):
+            g = t ^ (dt ^ side)
+            for j in range(SLOTS):
+                s = g * SLOTS + j
+                first = side * (SIDE + 1) + j * BLOCK
+                for y in range(YP):
+                    at = slice(y * LANES, (y + 1) * LANES)
+                    out_ref[first + y] = buf[s, q, :, at]
+                    out_ref[first + YP, y : y + 1, :] = jnp.where(
+                        q > 0, buf[s, below, SUB - 1 : SUB, at], buf[s, below, 0:1, at]
+                    )
+                    out_ref[first + YP + 1, y : y + 1, :] = jnp.where(
+                        q < quarters - 1, buf[s, above, 0:1, at], buf[s, above, SUB - 1 : SUB, at]
+                    )
+
+
+def pick(sends, bricks, weights, aperture, owners):
+    group = bricks.shape[0] // owners
+    quarters = bricks.shape[1]
+    return pl.pallas_call(
+        functools.partial(pick_kernel, sends, quarters, owners, group),
+        out_shape=[pltpu.VMEM((MESSAGE, SUB, LANES), jnp.float32) for _ in sends],
+        in_specs=[
+            pl.BlockSpec(memory_space=pltpu.SMEM),
+            pl.BlockSpec(memory_space=pltpu.SMEM),
+            pl.BlockSpec(memory_space=pltpu.HBM),
+        ],
+        out_specs=[pl.BlockSpec(memory_space=pltpu.VMEM) for _ in sends],
+        scratch_shapes=[
+            pltpu.VMEM((owners * SLOTS,) + bricks.shape[1:], jnp.float32),
+            pltpu.SemaphoreType.DMA((owners * SLOTS,)),
+        ],
+        compiler_params=pltpu.CompilerParams(vmem_limit_bytes=16 << 20),
+    )(aperture, weights, pltpu.with_memory_space_constraint(bricks, pltpu.HBM))
+
+
+def refine_side(ref, base, columns_ref, res_ref):
+    rows = lax.broadcasted_iota(jnp.int32, (SUB, LANES), 0)
+    turns = angular_rate / (2 * math.pi)
+    near, away = 0.75 * turns, 0.25 * turns
+    parts = []
+    for j in range(SLOTS):
+        even, odd = [], []
+        for y in range(YP):
+            first = base + j * BLOCK
+            c = ref[first + y]
+            low = jnp.broadcast_to(ref[first + YP, y : y + 1, :], c.shape)
+            high = jnp.broadcast_to(ref[first + YP + 1, y : y + 1, :], c.shape)
+            mid = near * c
+            even.append(mid + away * jnp.where(rows == 0, low, pltpu.roll(c, 1, 0)))
+            odd.append(mid + away * jnp.where(rows == SUB - 1, high, pltpu.roll(c, SUB - 1, 0)))
+        parts += even + odd
+    x = jnp.concatenate(parts, axis=0)
+    top = x.astype(jnp.bfloat16)
+    rest = (x - top.astype(jnp.float32)).astype(jnp.bfloat16)
+    res_ref[...] = jnp.dot(
+        jnp.concatenate([top, rest], axis=1), columns_ref[...], preferred_element_type=jnp.float32
+    )
+
+
+def add_slot(acc_ref, series, res_ref, j, weight, tile):
+    scaled = [weight * c for c in series]
+    for parity in range(2):
+
+        def part(pair, k):
+            r = ((j * 2 + parity) * YP + pair) * SUB
+            return res_ref[r : r + SUB, k * LANES : (k + 1) * LANES]
+
+        for y in range(FINE):
+            pair, k = divmod(y, 4)
+            if k == 0:
+                t = part(pair, 0) + (part(pair - 1, 3) if pair > 0 else part(pair, 2))
+            elif k == 1:
+                t = part(pair, 0) + part(pair, 3)
+            elif k == 2:
+                t = part(pair, 1) + part(pair, 2)
+            else:
+                t = part(pair, 1) + (part(pair + 1, 2) if pair < YP - 1 else part(pair, 3))
+            r = t - jnp.round(t)
+            u = r * r
+            p = scaled[5]
+            for c in scaled[4:0:-1]:
+                p = p * u + c
+            acc_ref[tile, parity, y] = acc_ref[tile, parity, y] + p * u
+
+
+def image_kernel(entries, rows, arrays, carried, sides, final, group, *refs):
+    ins, columns_ref, refs = refs[:arrays], refs[arrays], refs[arrays + 1 :]
+    old, refs = refs[:carried], refs[carried:]
+    if final:
+        out_ref, acc, refs = refs[0], refs[1:2], refs[2:]
+    else:
+        acc, refs = refs[:sides], refs[sides:]
+    bias, info, sem, res = refs[0], refs[1], refs[2], refs[3:]
+    copies = [
+        pltpu.make_async_copy(ins[which].at[tile, pl.ds(0, 1), :], info.at[k], sem.at[k])
+        for k, (which, tile) in enumerate(rows)
+    ]
+    for copy in copies:
+        copy.start()
+    series = cos_series()
+    refine_side(ins[entries[0][0]], entries[0][1], columns_ref, res[0])
+    for k in range(sides * group):
+        bias[k] = jnp.float32(0.0)
+    for copy in copies:
+        copy.wait()
+
+    def scalars(entry, j):
+        weight = info[entry[2], 0, entry[3] + 2 * j]
+        tile = info[entry[2], 0, entry[3] + 2 * j + 1].astype(jnp.int32)
+        return weight, tile
+
+    for entry in entries:
+        for j in range(SLOTS):
+            weight, tile = scalars(entry, j)
+            k = entry[4] * group + tile
+            bias[k] = bias[k] + weight * series[0]
+
+    for side in range(sides):
+        seeds = old if final else old[side : side + 1]
+
+        def seed(k, carry):
+            level = bias[side * group + k]
+            for parity in range(2):
+                for y in range(FINE):
+                    value = jnp.full((SUB, LANES), level, jnp.float32)
+                    for s in seeds:
+                        value = value + s[k, parity, y]
+                    acc[side][k, parity, y] = value
+            return carry
+
+        lax.fori_loop(0, group, seed, 0)
+
+    for n, entry in enumerate(entries):
+        if n + 1 < len(entries):
+            later = entries[n + 1]
+            refine_side(ins[later[0]], later[1], columns_ref, res[(n + 1) % 2])
+        for j in range(SLOTS):
+            weight, tile = scalars(entry, j)
+            add_slot(acc[entry[4]], series, res[n % 2], j, weight, tile)
+
+    if final:
+
+        def flush(k, carry):
+            for parity in range(2):
+                for y in range(FINE):
+                    start = k * (2 * SUB * FINE) + parity * FINE + y
+                    out_ref[pl.ds(start, SUB, stride=2 * FINE), :] = acc[0][k, parity, y]
+            return carry
+
+        lax.fori_loop(0, group, flush, 0)
+
+
+def image_step(messages, relayed, old, columns, group, final):
+    sides = 1 if final else 2
+    near = functools.partial(pltpu.with_memory_space_constraint, memory_space=pltpu.VMEM)
+    entries, arrays, rows = [], [], []
+    for m in messages:
+        for side in range(sides):
+            entries.append((len(arrays), side * (SIDE + 1), len(rows), side * 2 * SLOTS, side))
+        rows.append((len(arrays), SIDE))
+        arrays.append(m)
+    if relayed is not None:
+        for first in range(0, relayed.shape[0], SIDE + 1):
+            entries.append((len(arrays), first + 1, len(rows), 2 * SLOTS, 0))
+            rows.append((len(arrays), first))
+        arrays.append(relayed)
+    shape = (group, 2, FINE, SUB, LANES)
+    whole = pl.BlockSpec(memory_space=pltpu.VMEM)
+    scratch = [
+        pltpu.SMEM((sides * group,), jnp.float32),
+        pltpu.SMEM((len(rows), 1, LANES), jnp.float32),
+        pltpu.SemaphoreType.DMA((len(rows),)),
+        pltpu.VMEM((SLOTS * 2 * YP * SUB, 4 * LANES), jnp.float32),
+        pltpu.VMEM((SLOTS * 2 * YP * SUB, 4 * LANES), jnp.float32),
+    ]
+    if final:
+        out_shape = jax.ShapeDtypeStruct((group * 2 * SUB * FINE, LANES), jnp.float32)
+        out_specs = whole
+        scratch = [pltpu.VMEM(shape, jnp.float32)] + scratch
+    else:
+        out_shape = [pltpu.VMEM(shape, jnp.float32)] * 2
+        out_specs = [whole] * 2
+    return pl.pallas_call(
+        functools.partial(
+            image_kernel, entries, rows, len(arrays), len(old), sides, final, group
+        ),
+        out_shape=out_shape,
+        in_specs=[whole] * (len(arrays) + 1 + len(old)),
+        out_specs=out_specs,
+        scratch_shapes=scratch,
+        compiler_params=pltpu.CompilerParams(vmem_limit_bytes=16 << 20),
+    )(*[near(a) for a in arrays], near(columns), *[near(a) for a in old])
+
+
+def octet_shards(tables, weights, aperture):
+    quarters, owners = lax.axis_size("src"), lax.axis_size("tile")
+    group = tables.shape[1] // owners
+    columns = jnp.asarray(refine_columns(), jnp.bfloat16)
+    bricks = tables[0].reshape(-1, quarters, SUB, YP * LANES)
+
+    def permute(value, dz, dt):
+        def other(r, t):
+            return (r ^ dz) * owners + (t ^ dt)
+
+        pairs = [(r * owners + t, other(r, t)) for r in range(quarters) for t in range(owners)]
+        return lax.ppermute(value, ("src", "tile"), pairs)
+
+    chips = range(0, owners, 2)
+    lead = [(2, 0), (3, 0)]
+    near = [(0, dt) for dt in chips[1:]]
+    far = [(dz, dt) for dz in (2, 3) for dt in chips[1:]]
+    side = [(1, dt) for dt in chips]
+    order = lead + near + far + side
+    batches = [[(0, 0)] + near, lead + far[:2], far[2:], side[:-2], side[-2:]]
+    got = {}
+    sent = dict(zip(lead, pick(lead, bricks, weights, aperture, owners)))
+    rest = [(0, 0)] + order[len(lead) :]
+    sent.update(zip(rest, pick(rest, bricks, weights, aperture, owners)))
+    got[0, 0] = sent[0, 0]
+    for key in order:
+        got[key] = permute(sent[key], *key)
+    images = []
+    for batch in batches[:-1]:
+        messages = [got[key] for key in batch]
+        images = image_step(messages, None, images, columns, group, False)
+    mine, other = images
+    late = [got[key] for key in batches[-1]]
+    other = permute(other, 0, 1)
+    relayed = permute(jnp.concatenate([m[SIDE:] for m in late], axis=0), 0, 1)
+    image = image_step(late, relayed, [mine, other], columns, group, True)
+    return image.reshape(group, 2 * SUB, FINE, 2 * BZ)
 
 
 def solution(mesh):
@@ -88,6 +401,12 @@
         P(("src", "tile"), None),
         P(("src", "tile"), None),
     )
+    quarters, owners = mesh.shape["src"], mesh.shape["tile"]
+    fits = quarters == 4 and BX == quarters * SUB and owners == 8
     return jax.shard_map(
-        shards, mesh=mesh, in_specs=placed, out_specs=P("tile", "src", None, None), check_vma=False
-    )
+        octet_shards if fits else general_shards,
+        mesh=mesh,
+        in_specs=placed,
+        out_specs=P("tile", "src", None, None),
+        check_vma=False,
+    )

time: 570 us -> 93 us (0.16)
  local copies, waits for them, and re-layouts: 250 us -> 1.33 us
  matrix products: 97.6 us -> 0 us
  other arithmetic: 92.7 us -> 0.01 us
  waiting for transfers between devices: 103 us -> 40.6 us
  Pallas kernels: 0 us -> 20.6 us
  starting transfers between devices: 8.92 us -> 29 us
  between operations: 13.5 us -> 0.3 us
    dot_general x8 -> x0, matrix products: 97.6 us -> none  [one_block(): jnp.einsum('kp,kfyz->pfyz', select, phase, precision=lax.Precision.HIGHEST)]
    while x128 -> x0, local copies, waits for them, and re-layouts: 82 us -> none
    unnamed x2 -> x0, waiting for transfers between devices: 76.4 us -> none
    cos x8 -> x0, other arithmetic: 54 us -> none  [one_block(): phase = jnp.cos(angular_rate * fine)]
    slice x48 -> x2, local copies, waits for them, and re-layouts: 49.6 us -> 0.01 us  [octet_shards(): relayed = permute(jnp.concatenate([m[SIDE:] for m in late], axis=0), 0, 1)]
    mul x32 -> x0, local copies, waits for them, and re-layouts: 45.3 us -> none  [refine_axis(): even_rows = 0.75 * values + 0.25 * lower]
    ppermute x0 -> x17, waiting for transfers between devices: none -> 40.6 us  [permute(): return lax.ppermute(value, ('src', 'tile'), pairs)]
    ppermute x0 -> x17, starting transfers between devices: none -> 29 us  [permute(): return lax.ppermute(value, ('src', 'tile'), pairs)]
  transfers between devices with their start and end apart: 3 -> 17, of which waited for: 3 -> 7; matrix products, arithmetic and copies ran while one was open for 1% -> 0% of each run, Pallas kernels for 0% -> 13%
where the time goes in v2:
time: 93 us; the launch traced here: 91.8 us
  waiting for transfers between devices  40.6 us (44%)
  starting transfers between devices  29 us (31%)
  Pallas kernels  20.6 us (22%)
  local copies, waits for them, and re-layouts  1.33 us (1%)
    ppermute x17, waiting for transfers between devices, permute(): return lax.ppermute(value, ('src', 'tile'), pairs)  40.6 us
    ppermute x17, starting transfers between devices, permute(): return lax.ppermute(value, ('src', 'tile'), pairs)  29 us
    pallas_call x5, Pallas kernels, image_step(): pl.pallas_call(functools.partial(image_kernel, entries, rows, len(arrays)...  15.3 us
    pallas_call x2, Pallas kernels, pick(): pl.pallas_call(functools.partial(pick_kernel, sends, quarters, owners, gr...  5.27 us
  transfers between devices with their start and end apart: 17, of which 7 were waited for; matrix products, arithmetic and copies ran while one was open for 0% of the time, Pallas kernels for 13%

profile of v2, /device:TPU:0, one launch (start us, length us, event | category | flops | bytes accessed | tf_op | source)
XLA Modules:
  0.0 91.8 jit_solution(9634904383921879931)
XLA Ops:
  0.0 0.0 copy-start.1
  0.0 0.7 copy-done.1
  0.7 0.0 copy-start.2
  0.7 0.7 copy-done.2
  1.3 0.0 copy-start
  1.3 2.9 %shard_map.46 = (f32[41,8,128]{2,1,0:T(8,128)S(1)}, f32[41,8,128]{2,1,0:T(8,128)S(1)}, f32[41,8,128]{2,1,0:T(8,128)S(1)}, f32[41,8,128]{2,1,0:T(8,128)S(1)}, f32...) custom-call(s32[1,32]{1,0:T(1,128)S(1)} %copy-done.1, ...), custom_call_target="tpu_custom_call" | custom-call | tf_op jit(solution)/shard_map/pallas_call | solution.py:183
  4.2 3.0 %collective-permute-start.13 = (f32[41,8,128]{2,1,0:T(8,128)S(1)}, f32[41,8,128]{2,1,0:T(8,128)S(1)}, u32[]{:S(2)}, u32[]{:S(2)}) collective-permute-start(f32[41,8,128]{2,1,0:T(8,128)S(1)} %get-tuple-element.42), channel_id=1, source_target_pairs={{0,2},{1,3},{2,0},{3,1},{4,6},{5,7},{6,4},{7,5},{8,10},{9,11},{10,... | collective-permute-start | bytes 503816 | tf_op jit(solution)/shard_map/ppermute | solution.py:370
  7.2 1.5 %collective-permute-start.14 = (f32[41,8,128]{2,1,0:T(8,128)S(1)}, f32[41,8,128]{2,1,0:T(8,128)S(1)}, u32[]{:S(2)}, u32[]{:S(2)}) collective-permute-start(f32[41,8,128]{2,1,0:T(8,128)S(1)} %get-tuple-element.43), channel_id=1, source_target_pairs={{0,4},{1,5},{2,6},{3,7},{4,0},{5,1},{6,2},{7,3},{8,12},{9,13},{10,... | collective-permute-start | bytes 503816 | tf_op jit(solution)/shard_map/ppermute | solution.py:370
  8.8 0.0 collective-permute-start.15
  8.8 4.0 %collective-permute-start.11 = (f32[41,8,128]{2,1,0:T(8,128)S(1)}, f32[41,8,128]{2,1,0:T(8,128)S(1)}, u32[]{:S(2)}, u32[]{:S(2)}) collective-permute-start(f32[41,8,128]{2,1,0:T(8,128)S(1)} %get-tuple-element.39), channel_id=1, source_target_pairs={{0,18},{1,19},{2,16},{3,17},{4,22},{5,23},{6,20},{7,21},{8,26},{9,... | collective-permute-start | bytes 503816 | tf_op jit(solution)/shard_map/ppermute | solution.py:370
  12.8 1.3 %collective-permute-start.12 = (f32[41,8,128]{2,1,0:T(8,128)S(1)}, f32[41,8,128]{2,1,0:T(8,128)S(1)}, u32[]{:S(2)}, u32[]{:S(2)}) collective-permute-start(f32[41,8,128]{2,1,0:T(8,128)S(1)} %get-tuple-element.40), channel_id=1, source_target_pairs={{0,20},{1,21},{2,22},{3,23},{4,16},{5,17},{6,18},{7,19},{8,28},{9,... | collective-permute-start | bytes 503816 | tf_op jit(solution)/shard_map/ppermute | solution.py:370
  14.0 2.4 %shard_map.47 = (f32[41,8,128]{2,1,0:T(8,128)S(1)}, f32[41,8,128]{2,1,0:T(8,128)S(1)}) custom-call(s32[1,32]{1,0:T(1,128)S(1)} %copy-done.1, f32[1,32]{1,0:T(1,128)S(1)} %copy-done.2, f32[32,4,8,1024]{3,2,1,0:T(8,128)} %bitcast.3), custom_call_target="tpu_custom_call" | custom-call | tf_op jit(solution)/shard_map/pallas_call | solution.py:183
  16.4 0.0 collective-permute-done.13.refs_1_
  16.5 3.7 %collective-permute-start.10 = (f32[41,8,128]{2,1,0:T(8,128)S(1)}, f32[41,8,128]{2,1,0:T(8,128)S(1)}, u32[]{:S(2)}, u32[]{:S(2)}) collective-permute-start(f32[41,8,128]{2,1,0:T(8,128)S(1)} %get-tuple-element.38), channel_id=1, source_target_pairs={{0,24},{1,25},{2,26},{3,27},{4,28},{5,29},{6,30},{7,31},{8,16},{9,... | collective-permute-start | bytes 503816 | tf_op jit(solution)/shard_map/ppermute | solution.py:370
  20.1 0.0 collective-permute-done.14.refs_2_
  20.1 0.0 collective-permute-start.9
  20.1 0.0 collective-permute-done.15.refs_3_
  20.1 4.3 %collective-permute-start.5 = (f32[41,8,128]{2,1,0:T(8,128)S(1)}, f32[41,8,128]{2,1,0:T(8,128)S(1)}, u32[]{:S(2)}, u32[]{:S(2)}) collective-permute-start(f32[41,8,128]{2,1,0:T(8,128)S(1)} %get-tuple-element.33), channel_id=1, source_target_pairs={{0,22},{1,23},{2,20},{3,21},{4,18},{5,19},{6,16},{7,17},{8,30},{9,... | collective-permute-start | bytes 503816 | tf_op jit(solution)/shard_map/ppermute | solution.py:370
  24.4 10.9 %collective-permute-done.11.refs_2_ = f32[41,8,128]{2,1,0:T(8,128)S(1)} collective-permute-done((f32[41,8,128]{2,1,0:T(8,128)S(1)}, f32[41,8,128]{2,1,0:T(8,128)S(1)}, u32[]{:S(2)}, u32[]{:S(2)}) %collective-permute-start.11) | collective-permute-done | bytes 167968 | tf_op jit(solution)/shard_map/ppermute | solution.py:370
  35.3 3.4 %collective-permute-start.6 = (f32[41,8,128]{2,1,0:T(8,128)S(1)}, f32[41,8,128]{2,1,0:T(8,128)S(1)}, u32[]{:S(2)}, u32[]{:S(2)}) collective-permute-start(f32[41,8,128]{2,1,0:T(8,128)S(1)} %get-tuple-element.34), channel_id=1, source_target_pairs={{0,26},{1,27},{2,24},{3,25},{4,30},{5,31},{6,28},{7,29},{8,18},{9,... | collective-permute-start | bytes 503816 | tf_op jit(solution)/shard_map/ppermute | solution.py:370
  38.7 3.0 %collective-permute-done.12.refs_3_ = f32[41,8,128]{2,1,0:T(8,128)S(1)} collective-permute-done((f32[41,8,128]{2,1,0:T(8,128)S(1)}, f32[41,8,128]{2,1,0:T(8,128)S(1)}, u32[]{:S(2)}, u32[]{:S(2)}) %collective-permute-start.12) | collective-permute-done | bytes 167968 | tf_op jit(solution)/shard_map/ppermute | solution.py:370
  41.7 0.6 collective-permute-start.7
  42.3 0.0 collective-permute-done.10.refs_1_
  42.3 2.3 %collective-permute-start.8 = (f32[41,8,128]{2,1,0:T(8,128)S(1)}, f32[41,8,128]{2,1,0:T(8,128)S(1)}, u32[]{:S(2)}, u32[]{:S(2)}) collective-permute-start(f32[41,8,128]{2,1,0:T(8,128)S(1)} %get-tuple-element.36), channel_id=1, source_target_pairs={{0,30},{1,31},{2,28},{3,29},{4,26},{5,27},{6,24},{7,25},{8,22},{9,... | collective-permute-start | bytes 503816 | tf_op jit(solution)/shard_map/ppermute | solution.py:370
  44.6 12.3 %collective-permute-done.9.refs_0_ = f32[41,8,128]{2,1,0:T(8,128)S(1)} collective-permute-done((f32[41,8,128]{2,1,0:T(8,128)S(1)}, f32[41,8,128]{2,1,0:T(8,128)S(1)}, u32[]{:S(2)}, u32[]{:S(2)}) %collective-permute-start.9) | collective-permute-done | bytes 167968 | tf_op jit(solution)/shard_map/ppermute | solution.py:370
  56.9 0.0 collective-permute-start.3
  56.9 4.5 %collective-permute-done.5.refs_0_ = f32[41,8,128]{2,1,0:T(8,128)S(1)} collective-permute-done((f32[41,8,128]{2,1,0:T(8,128)S(1)}, f32[41,8,128]{2,1,0:T(8,128)S(1)}, u32[]{:S(2)}, u32[]{:S(2)}) %collective-permute-start.5) | collective-permute-done | bytes 167968 | tf_op jit(solution)/shard_map/ppermute | solution.py:370
  61.5 0.0 collective-permute-start.4
  61.5 0.0 copy-done
  61.5 3.3 %shard_map.48 = (f32[4,2,32,8,128]{4,3,2,1,0:T(8,128)S(1)}, f32[4,2,32,8,128]{4,3,2,1,0:T(8,128)S(1)}) custom-call(f32[41,8,128]{2,1,0:T(8,128)S(1)} %get-tuple-element.41.refs_0_, f32[41,8,128]{2,1,0:T(8,128)S(1)} %collective-permute-done.13.refs_1_, f32[41,8,128]{2,1,0:T(8,128)S(1)} %collective-permute-done.14.refs_2_, ...), custom_call_target="tpu_custom_call" | custom-call | tf_op jit(solution)/shard_map/pallas_call | solution.py:347
  64.8 3.2 %shard_map.49 = (f32[4,2,32,8,128]{4,3,2,1,0:T(8,128)S(1)}, f32[4,2,32,8,128]{4,3,2,1,0:T(8,128)S(1)}) custom-call(f32[41,8,128]{2,1,0:T(8,128)S(1)} %collective-permute-done.9.refs_0_, f32[41,8,128]{2,1,0:T(8,128)S(1)} %collective-permute-done.10.refs_1_, f32[41,8,128]{2,1,0:T(8,128)S(1)} %collective-permute-done.11.refs_2_, ...), custom_call_target="tpu_custom_call" | custom-call | tf_op jit(solution)/shard_map/pallas_call | solution.py:347
  68.0 0.0 collective-permute-done.6.refs_1_
  68.0 0.0 collective-permute-done.7.refs_2_
  68.0 0.0 collective-permute-done.8.refs_3_
  68.0 3.2 %shard_map.50 = (f32[4,2,32,8,128]{4,3,2,1,0:T(8,128)S(1)}, f32[4,2,32,8,128]{4,3,2,1,0:T(8,128)S(1)}) custom-call(f32[41,8,128]{2,1,0:T(8,128)S(1)} %collective-permute-done.5.refs_0_, f32[41,8,128]{2,1,0:T(8,128)S(1)} %collective-permute-done.6.refs_1_, f32[41,8,128]{2,1,0:T(8,128)S(1)} %collective-permute-done.7.refs_2_, ...), custom_call_target="tpu_custom_call" | custom-call | tf_op jit(solution)/shard_map/pallas_call | solution.py:347
  71.2 0.0 collective-permute-done.3.refs_0_
  71.2 0.0 collective-permute-done.4.refs_1_
  71.3 2.0 %shard_map.51 = (f32[4,2,32,8,128]{4,3,2,1,0:T(8,128)S(1)}, f32[4,2,32,8,128]{4,3,2,1,0:T(8,128)S(1)}) custom-call(f32[41,8,128]{2,1,0:T(8,128)S(1)} %collective-permute-done.3.refs_0_, f32[41,8,128]{2,1,0:T(8,128)S(1)} %collective-permute-done.4.refs_1_, bf16[256,512]{1,0:T(8,128)(2,1)S(1)} %copy-done, f32[4,2,32,8,128]{4,3,2,1,0:T(8,128)S(1)} %get-tuple-element.49.refs_3_, ...), custom_call_target="tpu_custom_call" | custom-call | tf_op jit(solution)/shard_map/pallas_call | solution.py:347
  73.3 0.1 collective-permute-start.16
  73.3 4.5 %collective-permute-start = (f32[41,8,128]{2,1,0:T(8,128)S(1)}, f32[41,8,128]{2,1,0:T(8,128)S(1)}, u32[]{:S(2)}, u32[]{:S(2)}) collective-permute-start(f32[41,8,128]{2,1,0:T(8,128)S(1)} %get-tuple-element.29), channel_id=1, source_target_pairs={{0,12},{1,13},{2,14},{3,15},{4,8},{5,9},{6,10},{7,11},{8,4},{9,5},... | collective-permute-start | bytes 503816 | tf_op jit(solution)/shard_map/ppermute | solution.py:370
  77.9 0.2 collective-permute-start.1
  78.1 4.9 %collective-permute-done.refs_0_ = f32[41,8,128]{2,1,0:T(8,128)S(1)} collective-permute-done((f32[41,8,128]{2,1,0:T(8,128)S(1)}, f32[41,8,128]{2,1,0:T(8,128)S(1)}, u32[]{:S(2)}, u32[]{:S(2)}) %collective-permute-start) | collective-permute-done | bytes 167968 | tf_op jit(solution)/shard_map/ppermute | solution.py:370
  83.0 3.5 %collective-permute-done.1.refs_1_ = f32[41,8,128]{2,1,0:T(8,128)S(1)} collective-permute-done((f32[41,8,128]{2,1,0:T(8,128)S(1)}, f32[41,8,128]{2,1,0:T(8,128)S(1)}, u32[]{:S(2)}, u32[]{:S(2)}) %collective-permute-start.1) | collective-permute-done | bytes 167968 | tf_op jit(solution)/shard_map/ppermute | solution.py:370
  86.6 0.1 collective-permute-start.2
  86.6 1.4 %collective-permute-done.2.refs_2_ = f32[42,8,128]{2,1,0:T(8,128)S(1)} collective-permute-done((f32[42,8,128]{2,1,0:T(8,128)S(1)}, f32[42,8,128]{2,1,0:T(8,128)S(1)}, u32[]{:S(2)}, u32[]{:S(2)}) %collective-permute-start.2) | collective-permute-done | bytes 172064 | tf_op jit(solution)/shard_map/ppermute | solution.py:370
  88.0 0.0 collective-permute-done.16.refs_5_
  88.0 3.6 %shard_map.52 = f32[2048,128]{1,0:T(8,128)} custom-call(f32[41,8,128]{2,1,0:T(8,128)S(1)} %collective-permute-done.refs_0_, f32[41,8,128]{2,1,0:T(8,128)S(1)} %collective-permute-done.1.refs_1_, f32[42,8,128]{2,1,0:T(8,128)S(1)} %collective-permute-done.2.refs_2_, bf16[256,512]{1,0:T(8,128)(2,1)S(1)} %copy-done, ...), custom_call_target="tpu_custom_call" | custom-call | tf_op jit(solution)/shard_map/pallas_call | solution.py:347
  (3 shorter events, 0.0 us)
Async XLA Ops:
  0.0 0.7 copy-start.1
  0.7 0.7 copy-start.2
  1.3 60.2 %copy-start = (bf16[256,512]{1,0:T(8,128)(2,1)S(1)}, bf16[256,512]{1,0:T(8,128)(2,1)}, u32[]{:S(2)}) copy-start(bf16[256,512]{1,0:T(8,128)(2,1)} %constant.2.clone.refs_4_.refs_2_.refs_3_) | copy-start | bytes 786436
  4.2 12.2 %collective-permute-start.13 = (f32[41,8,128]{2,1,0:T(8,128)S(1)}, f32[41,8,128]{2,1,0:T(8,128)S(1)}, u32[]{:S(2)}, u32[]{:S(2)}) collective-permute-start(f32[41,8,128]{2,1,0:T(8,128)S(1)} %get-tuple-element.42), channel_id=1, source_target_pairs={{0,2},{1,3},{2,0},{3,1},{4,6},{5,7},{6,4},{7,5},{8,10},{9,11},{10,... | collective-permute-start | bytes 503816 | tf_op jit(solution)/shard_map/ppermute | solution.py:370
  7.2 12.9 %collective-permute-start.14 = (f32[41,8,128]{2,1,0:T(8,128)S(1)}, f32[41,8,128]{2,1,0:T(8,128)S(1)}, u32[]{:S(2)}, u32[]{:S(2)}) collective-permute-start(f32[41,8,128]{2,1,0:T(8,128)S(1)} %get-tuple-element.43), channel_id=1, source_target_pairs={{0,4},{1,5},{2,6},{3,7},{4,0},{5,1},{6,2},{7,3},{8,12},{9,13},{10,... | collective-permute-start | bytes 503816 | tf_op jit(solution)/shard_map/ppermute | solution.py:370
  8.8 11.4 %collective-permute-start.15 = (f32[41,8,128]{2,1,0:T(8,128)S(1)}, f32[41,8,128]{2,1,0:T(8,128)S(1)}, u32[]{:S(2)}, u32[]{:S(2)}) collective-permute-start(f32[41,8,128]{2,1,0:T(8,128)S(1)} %get-tuple-element.44), channel_id=1, source_target_pairs={{0,6},{1,7},{2,4},{3,5},{4,2},{5,3},{6,0},{7,1},{8,14},{9,15},{10,... | collective-permute-start | bytes 503816 | tf_op jit(solution)/shard_map/ppermute | solution.py:370
  8.8 26.5 %collective-permute-start.11 = (f32[41,8,128]{2,1,0:T(8,128)S(1)}, f32[41,8,128]{2,1,0:T(8,128)S(1)}, u32[]{:S(2)}, u32[]{:S(2)}) collective-permute-start(f32[41,8,128]{2,1,0:T(8,128)S(1)} %get-tuple-element.39), channel_id=1, source_target_pairs={{0,18},{1,19},{2,16},{3,17},{4,22},{5,23},{6,20},{7,21},{8,26},{9,... | collective-permute-start | bytes 503816 | tf_op jit(solution)/shard_map/ppermute | solution.py:370
  12.8 29.0 %collective-permute-start.12 = (f32[41,8,128]{2,1,0:T(8,128)S(1)}, f32[41,8,128]{2,1,0:T(8,128)S(1)}, u32[]{:S(2)}, u32[]{:S(2)}) collective-permute-start(f32[41,8,128]{2,1,0:T(8,128)S(1)} %get-tuple-element.40), channel_id=1, source_target_pairs={{0,20},{1,21},{2,22},{3,23},{4,16},{5,17},{6,18},{7,19},{8,28},{9,... | collective-permute-start | bytes 503816 | tf_op jit(solution)/shard_map/ppermute | solution.py:370
  16.5 25.9 %collective-permute-start.10 = (f32[41,8,128]{2,1,0:T(8,128)S(1)}, f32[41,8,128]{2,1,0:T(8,128)S(1)}, u32[]{:S(2)}, u32[]{:S(2)}) collective-permute-start(f32[41,8,128]{2,1,0:T(8,128)S(1)} %get-tuple-element.38), channel_id=1, source_target_pairs={{0,24},{1,25},{2,26},{3,27},{4,28},{5,29},{6,30},{7,31},{8,16},{9,... | collective-permute-start | bytes 503816 | tf_op jit(solution)/shard_map/ppermute | solution.py:370
  20.1 36.8 %collective-permute-start.9 = (f32[41,8,128]{2,1,0:T(8,128)S(1)}, f32[41,8,128]{2,1,0:T(8,128)S(1)}, u32[]{:S(2)}, u32[]{:S(2)}) collective-permute-start(f32[41,8,128]{2,1,0:T(8,128)S(1)} %get-tuple-element.37), channel_id=1, source_target_pairs={{0,16},{1,17},{2,18},{3,19},{4,20},{5,21},{6,22},{7,23},{8,24},{9,... | collective-permute-start | bytes 503816 | tf_op jit(solution)/shard_map/ppermute | solution.py:370
  20.1 41.3 %collective-permute-start.5 = (f32[41,8,128]{2,1,0:T(8,128)S(1)}, f32[41,8,128]{2,1,0:T(8,128)S(1)}, u32[]{:S(2)}, u32[]{:S(2)}) collective-permute-start(f32[41,8,128]{2,1,0:T(8,128)S(1)} %get-tuple-element.33), channel_id=1, source_target_pairs={{0,22},{1,23},{2,20},{3,21},{4,18},{5,19},{6,16},{7,17},{8,30},{9,... | collective-permute-start | bytes 503816 | tf_op jit(solution)/shard_map/ppermute | solution.py:370
  35.3 32.7 %collective-permute-start.6 = (f32[41,8,128]{2,1,0:T(8,128)S(1)}, f32[41,8,128]{2,1,0:T(8,128)S(1)}, u32[]{:S(2)}, u32[]{:S(2)}) collective-permute-start(f32[41,8,128]{2,1,0:T(8,128)S(1)} %get-tuple-element.34), channel_id=1, source_target_pairs={{0,26},{1,27},{2,24},{3,25},{4,30},{5,31},{6,28},{7,29},{8,18},{9,... | collective-permute-start | bytes 503816 | tf_op jit(solution)/shard_map/ppermute | solution.py:370
  41.7 26.3 %collective-permute-start.7 = (f32[41,8,128]{2,1,0:T(8,128)S(1)}, f32[41,8,128]{2,1,0:T(8,128)S(1)}, u32[]{:S(2)}, u32[]{:S(2)}) collective-permute-start(f32[41,8,128]{2,1,0:T(8,128)S(1)} %get-tuple-element.35), channel_id=1, source_target_pairs={{0,28},{1,29},{2,30},{3,31},{4,24},{5,25},{6,26},{7,27},{8,20},{9,... | collective-permute-start | bytes 503816 | tf_op jit(solution)/shard_map/ppermute | solution.py:370
  42.3 25.7 %collective-permute-start.8 = (f32[41,8,128]{2,1,0:T(8,128)S(1)}, f32[41,8,128]{2,1,0:T(8,128)S(1)}, u32[]{:S(2)}, u32[]{:S(2)}) collective-permute-start(f32[41,8,128]{2,1,0:T(8,128)S(1)} %get-tuple-element.36), channel_id=1, source_target_pairs={{0,30},{1,31},{2,28},{3,29},{4,26},{5,27},{6,24},{7,25},{8,22},{9,... | collective-permute-start | bytes 503816 | tf_op jit(solution)/shard_map/ppermute | solution.py:370
  56.9 14.3 %collective-permute-start.3 = (f32[41,8,128]{2,1,0:T(8,128)S(1)}, f32[41,8,128]{2,1,0:T(8,128)S(1)}, u32[]{:S(2)}, u32[]{:S(2)}) collective-permute-start(f32[41,8,128]{2,1,0:T(8,128)S(1)} %get-tuple-element.31), channel_id=1, source_target_pairs={{0,8},{1,9},{2,10},{3,11},{4,12},{5,13},{6,14},{7,15},{8,0},{9,1},... | collective-permute-start | bytes 503816 | tf_op jit(solution)/shard_map/ppermute | solution.py:370
  61.5 9.8 %collective-permute-start.4 = (f32[41,8,128]{2,1,0:T(8,128)S(1)}, f32[41,8,128]{2,1,0:T(8,128)S(1)}, u32[]{:S(2)}, u32[]{:S(2)}) collective-permute-start(f32[41,8,128]{2,1,0:T(8,128)S(1)} %get-tuple-element.32), channel_id=1, source_target_pairs={{0,10},{1,11},{2,8},{3,9},{4,14},{5,15},{6,12},{7,13},{8,2},{9,3},... | collective-permute-start | bytes 503816 | tf_op jit(solution)/shard_map/ppermute | solution.py:370
  73.3 14.8 %collective-permute-start.16 = (f32[4,2,32,8,128]{4,3,2,1,0:T(8,128)S(1)}, f32[4,2,32,8,128]{4,3,2,1,0:T(8,128)S(1)}, u32[]{:S(2)}, u32[]{:S(2)}) collective-permute-start(f32[4,2,32,8,128]{4,3,2,1,0:T(8,128)S(1)} %get-tuple-element.52), channel_id=1, source_target_pairs={{0,1},{1,0},{2,3},{3,2},{4,5},{5,4},{6,7},{7,6},{8,9},{9,8},{10,11... | collective-permute-start | bytes 3145736 | tf_op jit(solution)/shard_map/ppermute | solution.py:370
  73.3 9.7 %collective-permute-start = (f32[41,8,128]{2,1,0:T(8,128)S(1)}, f32[41,8,128]{2,1,0:T(8,128)S(1)}, u32[]{:S(2)}, u32[]{:S(2)}) collective-permute-start(f32[41,8,128]{2,1,0:T(8,128)S(1)} %get-tuple-element.29), channel_id=1, source_target_pairs={{0,12},{1,13},{2,14},{3,15},{4,8},{5,9},{6,10},{7,11},{8,4},{9,5},... | collective-permute-start | bytes 503816 | tf_op jit(solution)/shard_map/ppermute | solution.py:370
  77.9 8.6 %collective-permute-start.1 = (f32[41,8,128]{2,1,0:T(8,128)S(1)}, f32[41,8,128]{2,1,0:T(8,128)S(1)}, u32[]{:S(2)}, u32[]{:S(2)}) collective-permute-start(f32[41,8,128]{2,1,0:T(8,128)S(1)} %get-tuple-element.30), channel_id=1, source_target_pairs={{0,14},{1,15},{2,12},{3,13},{4,10},{5,11},{6,8},{7,9},{8,6},{9,7},... | collective-permute-start | bytes 503816 | tf_op jit(solution)/shard_map/ppermute | solution.py:370
  86.6 1.5 %collective-permute-start.2 = (f32[42,8,128]{2,1,0:T(8,128)S(1)}, f32[42,8,128]{2,1,0:T(8,128)S(1)}, u32[]{:S(2)}, u32[]{:S(2)}) collective-permute-start(f32[42,8,128]{2,1,0:T(8,128)S(1)} %pad_maximum_fusion), channel_id=1, source_target_pairs={{0,1},{1,0},{2,3},{3,2},{4,5},{5,4},{6,7},{7,6},{8,9},{9,8},{10,11... | collective-permute-start | bytes 516104 | tf_op jit(solution)/shard_map/ppermute | solution.py:370

commit v3 on v2

--- a/solution.py
+++ b/solution.py
@@ -134,24 +134,34 @@
     return local, weight
 
 
-def pick_kernel(sends, quarters, owners, group, mask_ref, weight_ref, tables_ref, *refs):
-    outs, (buf, sem) = refs[: len(sends)], refs[len(sends) :]
-    copies = []
-    for g in range(owners):
+def pick_kernel(sends, quarters, group, mask_in, weight_in, tables_ref, *refs):
+    outs, (mask_ref, weight_ref, small, buf, sem) = refs[: len(sends)], refs[len(sends) :]
+    heads = [
+        pltpu.make_async_copy(mask_in, mask_ref, small.at[0]),
+        pltpu.make_async_copy(weight_in, weight_ref, small.at[1]),
+    ]
+    for head in heads:
+        head.start()
+    for head in heads:
+        head.wait()
+    r, t = lax.axis_index("src"), lax.axis_index("tile")
+    lanes = lax.broadcasted_iota(jnp.int32, (SUB, LANES), 1)
+    offsets = sorted({dt ^ side for _, dt in sends for side in range(2)})
+    found, copies = {}, []
+    for n, offset in enumerate(offsets):
+        g = t ^ offset
         for j in range(SLOTS):
-            local, _ = slot_scalars(mask_ref, weight_ref, g * group, group, j)
-            s = g * SLOTS + j
+            local, weight = slot_scalars(mask_ref, weight_ref, g * group, group, j)
+            found[offset, j] = (n * SLOTS + j, local, weight)
+            s = n * SLOTS + j
             copy = pltpu.make_async_copy(tables_ref.at[g * group + local], buf.at[s], sem.at[s])
             copy.start()
             copies.append(copy)
-    r, t = lax.axis_index("src"), lax.axis_index("tile")
-    lanes = lax.broadcasted_iota(jnp.int32, (SUB, LANES), 1)
     for out_ref, (dz, dt) in zip(outs, sends):
         info = jnp.zeros((SUB, LANES), jnp.float32)
         for side in range(2):
-            g = t ^ (dt ^ side)
             for j in range(SLOTS):
-                local, weight = slot_scalars(mask_ref, weight_ref, g * group, group, j)
+                _, local, weight = found[dt ^ side, j]
                 lane = 2 * (side * SLOTS + j)
                 info = jnp.where(lanes == lane, weight, info)
                 info = jnp.where(lanes == lane + 1, local.astype(jnp.float32), info)
@@ -162,9 +172,8 @@
         q = r ^ dz
         below, above = jnp.maximum(q - 1, 0), jnp.minimum(q + 1, quarters - 1)
         for side in range(2):
-            g = t ^ (dt ^ side)
             for j in range(SLOTS):
-                s = g * SLOTS + j
+                s = found[dt ^ side, j][0]
                 first = side * (SIDE + 1) + j * BLOCK
                 for y in range(YP):
                     at = slice(y * LANES, (y + 1) * LANES)
@@ -180,21 +189,22 @@
 def pick(sends, bricks, weights, aperture, owners):
     group = bricks.shape[0] // owners
     quarters = bricks.shape[1]
+    slots = SLOTS * len({dt ^ side for _, dt in sends for side in range(2)})
+    home = functools.partial(pltpu.with_memory_space_constraint, memory_space=pltpu.HBM)
     return pl.pallas_call(
-        functools.partial(pick_kernel, sends, quarters, owners, group),
+        functools.partial(pick_kernel, sends, quarters, group),
         out_shape=[pltpu.VMEM((MESSAGE, SUB, LANES), jnp.float32) for _ in sends],
-        in_specs=[
-            pl.BlockSpec(memory_space=pltpu.SMEM),
-            pl.BlockSpec(memory_space=pltpu.SMEM),
-            pl.BlockSpec(memory_space=pltpu.HBM),
-        ],
+        in_specs=[pl.BlockSpec(memory_space=pltpu.HBM)] * 3,
         out_specs=[pl.BlockSpec(memory_space=pltpu.VMEM) for _ in sends],
         scratch_shapes=[
-            pltpu.VMEM((owners * SLOTS,) + bricks.shape[1:], jnp.float32),
-            pltpu.SemaphoreType.DMA((owners * SLOTS,)),
+            pltpu.SMEM(aperture.shape, aperture.dtype),
+            pltpu.SMEM(weights.shape, weights.dtype),
+            pltpu.SemaphoreType.DMA((2,)),
+            pltpu.VMEM((slots,) + bricks.shape[1:], jnp.float32),
+            pltpu.SemaphoreType.DMA((slots,)),
         ],
         compiler_params=pltpu.CompilerParams(vmem_limit_bytes=16 << 20),
-    )(aperture, weights, pltpu.with_memory_space_constraint(bricks, pltpu.HBM))
+    )(home(aperture), home(weights), home(bricks))
 
 
 def refine_side(ref, base, columns_ref, res_ref):
@@ -242,19 +252,22 @@
             r = t - jnp.round(t)
             u = r * r
             p = scaled[5]
-            for c in scaled[4:0:-1]:
+            for c in scaled[4::-1]:
                 p = p * u + c
-            acc_ref[tile, parity, y] = acc_ref[tile, parity, y] + p * u
-
-
-def image_kernel(entries, rows, arrays, carried, sides, final, group, *refs):
+            at = slice((parity * FINE + y) * SUB, (parity * FINE + y + 1) * SUB)
+            acc_ref[tile, at, :] = acc_ref[tile, at, :] + p
+
+
+def image_kernel(entries, rows, arrays, sides, first, final, group, *refs):
     ins, columns_ref, refs = refs[:arrays], refs[arrays], refs[arrays + 1 :]
-    old, refs = refs[:carried], refs[carried:]
     if final:
+        other_ref, refs = refs[1], refs[2:]
         out_ref, acc, refs = refs[0], refs[1:2], refs[2:]
+        stage, out_sem, refs = refs[0], refs[1], refs[2:]
     else:
+        refs = refs if first else refs[sides:]
         acc, refs = refs[:sides], refs[sides:]
-    bias, info, sem, res = refs[0], refs[1], refs[2], refs[3:]
+    info, sem, res = refs[0], refs[1], refs[2:]
     copies = [
         pltpu.make_async_copy(ins[which].at[tile, pl.ds(0, 1), :], info.at[k], sem.at[k])
         for k, (which, tile) in enumerate(rows)
@@ -263,59 +276,42 @@
         copy.start()
     series = cos_series()
     refine_side(ins[entries[0][0]], entries[0][1], columns_ref, res[0])
-    for k in range(sides * group):
-        bias[k] = jnp.float32(0.0)
+    if first:
+        for image in acc:
+
+            def clear(k, carry):
+                image[k] = jnp.zeros(image.shape[1:], jnp.float32)
+                return carry
+
+            lax.fori_loop(0, group, clear, 0)
     for copy in copies:
         copy.wait()
-
-    def scalars(entry, j):
-        weight = info[entry[2], 0, entry[3] + 2 * j]
-        tile = info[entry[2], 0, entry[3] + 2 * j + 1].astype(jnp.int32)
-        return weight, tile
-
-    for entry in entries:
-        for j in range(SLOTS):
-            weight, tile = scalars(entry, j)
-            k = entry[4] * group + tile
-            bias[k] = bias[k] + weight * series[0]
-
-    for side in range(sides):
-        seeds = old if final else old[side : side + 1]
-
-        def seed(k, carry):
-            level = bias[side * group + k]
-            for parity in range(2):
-                for y in range(FINE):
-                    value = jnp.full((SUB, LANES), level, jnp.float32)
-                    for s in seeds:
-                        value = value + s[k, parity, y]
-                    acc[side][k, parity, y] = value
-            return carry
-
-        lax.fori_loop(0, group, seed, 0)
-
     for n, entry in enumerate(entries):
         if n + 1 < len(entries):
             later = entries[n + 1]
             refine_side(ins[later[0]], later[1], columns_ref, res[(n + 1) % 2])
         for j in range(SLOTS):
-            weight, tile = scalars(entry, j)
+            weight = info[entry[2], 0, entry[3] + 2 * j]
+            tile = info[entry[2], 0, entry[3] + 2 * j + 1].astype(jnp.int32)
             add_slot(acc[entry[4]], series, res[n % 2], j, weight, tile)
 
     if final:
-
-        def flush(k, carry):
+        written = []
+        for k in range(group):
             for parity in range(2):
-                for y in range(FINE):
-                    start = k * (2 * SUB * FINE) + parity * FINE + y
-                    out_ref[pl.ds(start, SUB, stride=2 * FINE), :] = acc[0][k, parity, y]
-            return carry
-
-        lax.fori_loop(0, group, flush, 0)
-
-
-def image_step(messages, relayed, old, columns, group, final):
-    sides = 1 if final else 2
+                for x in range(SUB):
+                    for y in range(0, FINE, SUB):
+                        at = pl.ds((parity * FINE + y) * SUB + x, SUB, stride=SUB)
+                        row = (2 * x + parity) * FINE + y
+                        stage[k, row : row + SUB, :] = acc[0][k, at, :] + other_ref[k, at, :]
+            copy = pltpu.make_async_copy(stage.at[k], out_ref.at[k], out_sem.at[k])
+            copy.start()
+            written.append(copy)
+        for copy in written:
+            copy.wait()
+
+
+def image_step(messages, relayed, images, columns, group, final=False, sides=2):
     near = functools.partial(pltpu.with_memory_space_constraint, memory_space=pltpu.VMEM)
     entries, arrays, rows = [], [], []
     for m in messages:
@@ -328,32 +324,35 @@
             entries.append((len(arrays), first + 1, len(rows), 2 * SLOTS, 0))
             rows.append((len(arrays), first))
         arrays.append(relayed)
-    shape = (group, 2, FINE, SUB, LANES)
+    shape = (group, 2 * FINE * SUB, LANES)
     whole = pl.BlockSpec(memory_space=pltpu.VMEM)
     scratch = [
-        pltpu.SMEM((sides * group,), jnp.float32),
         pltpu.SMEM((len(rows), 1, LANES), jnp.float32),
         pltpu.SemaphoreType.DMA((len(rows),)),
         pltpu.VMEM((SLOTS * 2 * YP * SUB, 4 * LANES), jnp.float32),
         pltpu.VMEM((SLOTS * 2 * YP * SUB, 4 * LANES), jnp.float32),
     ]
+    kept = len(arrays) + 1
     if final:
-        out_shape = jax.ShapeDtypeStruct((group * 2 * SUB * FINE, LANES), jnp.float32)
-        out_specs = whole
-        scratch = [pltpu.VMEM(shape, jnp.float32)] + scratch
+        out_shape = [jax.ShapeDtypeStruct(shape, jnp.float32), pltpu.VMEM(shape, jnp.float32)]
+        out_specs = [pl.BlockSpec(memory_space=pltpu.HBM), whole]
+        scratch = [pltpu.VMEM(shape, jnp.float32), pltpu.SemaphoreType.DMA((group,))] + scratch
+        aliases = {kept: 1}
     else:
-        out_shape = [pltpu.VMEM(shape, jnp.float32)] * 2
-        out_specs = [whole] * 2
+        out_shape = [pltpu.VMEM(shape, jnp.float32)] * sides
+        out_specs = [whole] * sides
+        aliases = {kept + k: k for k in range(len(images))}
     return pl.pallas_call(
         functools.partial(
-            image_kernel, entries, rows, len(arrays), len(old), sides, final, group
+            image_kernel, entries, rows, len(arrays), sides, not images, final, group
         ),
         out_shape=out_shape,
-        in_specs=[whole] * (len(arrays) + 1 + len(old)),
+        in_specs=[whole] * (kept + len(images)),
         out_specs=out_specs,
         scratch_shapes=scratch,
+        input_output_aliases=aliases,
         compiler_params=pltpu.CompilerParams(vmem_limit_bytes=16 << 20),
-    )(*[near(a) for a in arrays], near(columns), *[near(a) for a in old])
+    )(*[near(a) for a in arrays], near(columns), *[near(a) for a in images])
 
 
 def octet_shards(tables, weights, aperture):
@@ -375,7 +374,15 @@
     far = [(dz, dt) for dz in (2, 3) for dt in chips[1:]]
     side = [(1, dt) for dt in chips]
     order = lead + near + far + side
-    batches = [[(0, 0)] + near, lead + far[:2], far[2:], side[:-2], side[-2:]]
+    batches = [
+        [(0, 0)] + near,
+        lead,
+        [(2, 2), (2, 4)],
+        [(2, 6), (3, 2)],
+        [(1, 0), (1, 2)],
+        [(3, 4), (1, 4)],
+    ]
+    last = [(3, 6), (1, 6)]
     got = {}
     sent = dict(zip(lead, pick(lead, bricks, weights, aperture, owners)))
     rest = [(0, 0)] + order[len(lead) :]
@@ -384,14 +391,15 @@
     for key in order:
         got[key] = permute(sent[key], *key)
     images = []
-    for batch in batches[:-1]:
+    for batch in batches:
         messages = [got[key] for key in batch]
-        images = image_step(messages, None, images, columns, group, False)
+        images = image_step(messages, None, images, columns, group)
     mine, other = images
-    late = [got[key] for key in batches[-1]]
+    late = [got[key] for key in last]
     other = permute(other, 0, 1)
     relayed = permute(jnp.concatenate([m[SIDE:] for m in late], axis=0), 0, 1)
-    image = image_step(late, relayed, [mine, other], columns, group, True)
+    (mine,) = image_step(late, None, [mine], columns, group, sides=1)
+    image, _ = image_step([], relayed, [mine, other], columns, group, final=True, sides=1)
     return image.reshape(group, 2 * SUB, FINE, 2 * BZ)
 
 

time: 93 us -> 88.9 us (0.956); the launches traced: 91.8 us -> 88.7 us
  local copies, waits for them, and re-layouts: 1.33 us -> 0.02 us
    unnamed x6 -> x2, local copies, waits for them, and re-layouts: 1.31 us -> 0.01 us
    pallas_call x5 -> x8, Pallas kernels: 15.3 us -> 15.7 us  [image_step(): pl.pallas_call(functools.partial(image_kernel, entries, rows, len(arrays)...]
  transfers between devices with their start and end apart: 17 -> 17, of which waited for: 7 -> 7; matrix products, arithmetic and copies ran while one was open for 0% -> 0% of each run, Pallas kernels for 13% -> 15%
where the time goes in v3:
time: 88.9 us; the launch traced here: 88.7 us
  waiting for transfers between devices  39.7 us (45%)
  starting transfers between devices  28.1 us (32%)
  Pallas kernels  20.8 us (23%)
    ppermute x17, waiting for transfers between devices, permute(): return lax.ppermute(value, ('src', 'tile'), pairs)  39.7 us
    ppermute x17, starting transfers between devices, permute(): return lax.ppermute(value, ('src', 'tile'), pairs)  28.1 us
    pallas_call x8, Pallas kernels, image_step(): pl.pallas_call(functools.partial(image_kernel, entries, rows, len(arrays)...  15.7 us
    pallas_call x2, Pallas kernels, pick(): pl.pallas_call(functools.partial(pick_kernel, sends, quarters, group), ou...  5.1 us
  transfers between devices with their start and end apart: 17, of which 7 were waited for; matrix products, arithmetic and copies ran while one was open for 0% of the time, Pallas kernels for 15%

profile of v3, /device:TPU:0, one launch (start us, length us, event | category | flops | bytes accessed | tf_op | source)
XLA Modules:
  0.0 88.7 jit_solution(9650276039312232097)
XLA Ops:
  0.0 0.0 copy-start
  0.0 3.2 %shard_map.46 = (f32[41,8,128]{2,1,0:T(8,128)S(1)}, f32[41,8,128]{2,1,0:T(8,128)S(1)}, f32[41,8,128]{2,1,0:T(8,128)S(1)}, f32[41,8,128]{2,1,0:T(8,128)S(1)}, f32...) custom-call(s32[1,32]{1,0:T(1,128)} %mask_in.3, ...), custom_call_target="tpu_custom_call" | custom-call | tf_op jit(solution)/shard_map/pallas_call | solution.py:194
  3.2 3.0 %collective-permute-start.13 = (f32[41,8,128]{2,1,0:T(8,128)S(1)}, f32[41,8,128]{2,1,0:T(8,128)S(1)}, u32[]{:S(2)}, u32[]{:S(2)}) collective-permute-start(f32[41,8,128]{2,1,0:T(8,128)S(1)} %get-tuple-element.47), channel_id=1, source_target_pairs={{0,2},{1,3},{2,0},{3,1},{4,6},{5,7},{6,4},{7,5},{8,10},{9,11},{10,... | collective-permute-start | bytes 503816 | tf_op jit(solution)/shard_map/ppermute | solution.py:369
  6.2 1.5 %collective-permute-start.14 = (f32[41,8,128]{2,1,0:T(8,128)S(1)}, f32[41,8,128]{2,1,0:T(8,128)S(1)}, u32[]{:S(2)}, u32[]{:S(2)}) collective-permute-start(f32[41,8,128]{2,1,0:T(8,128)S(1)} %get-tuple-element.48), channel_id=1, source_target_pairs={{0,4},{1,5},{2,6},{3,7},{4,0},{5,1},{6,2},{7,3},{8,12},{9,13},{10,... | collective-permute-start | bytes 503816 | tf_op jit(solution)/shard_map/ppermute | solution.py:369
  7.7 0.0 collective-permute-start.15
  7.8 1.9 %shard_map.47 = (f32[41,8,128]{2,1,0:T(8,128)S(1)}, f32[41,8,128]{2,1,0:T(8,128)S(1)}) custom-call(s32[1,32]{1,0:T(1,128)} %mask_in.3, f32[1,32]{1,0:T(1,128)} %weight_in.3, f32[32,4,8,1024]{3,2,1,0:T(8,128)} %bitcast.3), custom_call_target="tpu_custom_call" | custom-call | tf_op jit(solution)/shard_map/pallas_call | solution.py:194
  9.7 3.1 %collective-permute-start.11 = (f32[41,8,128]{2,1,0:T(8,128)S(1)}, f32[41,8,128]{2,1,0:T(8,128)S(1)}, u32[]{:S(2)}, u32[]{:S(2)}) collective-permute-start(f32[41,8,128]{2,1,0:T(8,128)S(1)} %get-tuple-element.44), channel_id=1, source_target_pairs={{0,16},{1,17},{2,18},{3,19},{4,20},{5,21},{6,22},{7,23},{8,24},{9,... | collective-permute-start | bytes 503816 | tf_op jit(solution)/shard_map/ppermute | solution.py:369
  12.8 1.3 %collective-permute-start.12 = (f32[41,8,128]{2,1,0:T(8,128)S(1)}, f32[41,8,128]{2,1,0:T(8,128)S(1)}, u32[]{:S(2)}, u32[]{:S(2)}) collective-permute-start(f32[41,8,128]{2,1,0:T(8,128)S(1)} %get-tuple-element.45), channel_id=1, source_target_pairs={{0,24},{1,25},{2,26},{3,27},{4,28},{5,29},{6,30},{7,31},{8,16},{9,... | collective-permute-start | bytes 503816 | tf_op jit(solution)/shard_map/ppermute | solution.py:369
  14.2 0.0 collective-permute-done.13.refs_1_
  14.2 2.6 %collective-permute-start.10 = (f32[41,8,128]{2,1,0:T(8,128)S(1)}, f32[41,8,128]{2,1,0:T(8,128)S(1)}, u32[]{:S(2)}, u32[]{:S(2)}) collective-permute-start(f32[41,8,128]{2,1,0:T(8,128)S(1)} %get-tuple-element.43), channel_id=1, source_target_pairs={{0,20},{1,21},{2,22},{3,23},{4,16},{5,17},{6,18},{7,19},{8,28},{9,... | collective-permute-start | bytes 503816 | tf_op jit(solution)/shard_map/ppermute | solution.py:369
  16.8 0.0 collective-permute-done.14.refs_2_
  16.8 2.2 %collective-permute-start.9 = (f32[41,8,128]{2,1,0:T(8,128)S(1)}, f32[41,8,128]{2,1,0:T(8,128)S(1)}, u32[]{:S(2)}, u32[]{:S(2)}) collective-permute-start(f32[41,8,128]{2,1,0:T(8,128)S(1)} %get-tuple-element.42), channel_id=1, source_target_pairs={{0,18},{1,19},{2,16},{3,17},{4,22},{5,23},{6,20},{7,21},{8,26},{9,... | collective-permute-start | bytes 503816 | tf_op jit(solution)/shard_map/ppermute | solution.py:369
  19.0 0.0 collective-permute-done.15.refs_3_
  19.0 1.6 %collective-permute-start.7 = (f32[41,8,128]{2,1,0:T(8,128)S(1)}, f32[41,8,128]{2,1,0:T(8,128)S(1)}, u32[]{:S(2)}, u32[]{:S(2)}) collective-permute-start(f32[41,8,128]{2,1,0:T(8,128)S(1)} %get-tuple-element.40), channel_id=1, source_target_pairs={{0,22},{1,23},{2,20},{3,21},{4,18},{5,19},{6,16},{7,17},{8,30},{9,... | collective-permute-start | bytes 503816 | tf_op jit(solution)/shard_map/ppermute | solution.py:369
  20.6 14.8 %collective-permute-done.11.refs_0_ = f32[41,8,128]{2,1,0:T(8,128)S(1)} collective-permute-done((f32[41,8,128]{2,1,0:T(8,128)S(1)}, f32[41,8,128]{2,1,0:T(8,128)S(1)}, u32[]{:S(2)}, u32[]{:S(2)}) %collective-permute-start.11) | collective-permute-done | bytes 167968 | tf_op jit(solution)/shard_map/ppermute | solution.py:369
  35.4 3.4 %collective-permute-start.8 = (f32[41,8,128]{2,1,0:T(8,128)S(1)}, f32[41,8,128]{2,1,0:T(8,128)S(1)}, u32[]{:S(2)}, u32[]{:S(2)}) collective-permute-start(f32[41,8,128]{2,1,0:T(8,128)S(1)} %get-tuple-element.41), channel_id=1, source_target_pairs={{0,26},{1,27},{2,24},{3,25},{4,30},{5,31},{6,28},{7,29},{8,18},{9,... | collective-permute-start | bytes 503816 | tf_op jit(solution)/shard_map/ppermute | solution.py:369
  38.8 0.0 collective-permute-done.12.refs_1_
  38.8 2.6 %collective-permute-start.5 = (f32[41,8,128]{2,1,0:T(8,128)S(1)}, f32[41,8,128]{2,1,0:T(8,128)S(1)}, u32[]{:S(2)}, u32[]{:S(2)}) collective-permute-start(f32[41,8,128]{2,1,0:T(8,128)S(1)} %get-tuple-element.38), channel_id=1, source_target_pairs={{0,8},{1,9},{2,10},{3,11},{4,12},{5,13},{6,14},{7,15},{8,0},{9,1},... | collective-permute-start | bytes 503816 | tf_op jit(solution)/shard_map/ppermute | solution.py:369
  41.4 5.9 %collective-permute-done.10.refs_1_ = f32[41,8,128]{2,1,0:T(8,128)S(1)} collective-permute-done((f32[41,8,128]{2,1,0:T(8,128)S(1)}, f32[41,8,128]{2,1,0:T(8,128)S(1)}, u32[]{:S(2)}, u32[]{:S(2)}) %collective-permute-start.10) | collective-permute-done | bytes 167968 | tf_op jit(solution)/shard_map/ppermute | solution.py:369
  47.3 0.0 collective-permute-start.6
  47.3 3.5 %collective-permute-done.9.refs_0_ = f32[41,8,128]{2,1,0:T(8,128)S(1)} collective-permute-done((f32[41,8,128]{2,1,0:T(8,128)S(1)}, f32[41,8,128]{2,1,0:T(8,128)S(1)}, u32[]{:S(2)}, u32[]{:S(2)}) %collective-permute-start.9) | collective-permute-done | bytes 167968 | tf_op jit(solution)/shard_map/ppermute | solution.py:369
  50.7 3.5 %collective-permute-start.3 = (f32[41,8,128]{2,1,0:T(8,128)S(1)}, f32[41,8,128]{2,1,0:T(8,128)S(1)}, u32[]{:S(2)}, u32[]{:S(2)}) collective-permute-start(f32[41,8,128]{2,1,0:T(8,128)S(1)} %get-tuple-element.36), channel_id=1, source_target_pairs={{0,28},{1,29},{2,30},{3,31},{4,24},{5,25},{6,26},{7,27},{8,20},{9,... | collective-permute-start | bytes 503816 | tf_op jit(solution)/shard_map/ppermute | solution.py:369
  54.3 4.3 %collective-permute-done.7.refs_0_ = f32[41,8,128]{2,1,0:T(8,128)S(1)} collective-permute-done((f32[41,8,128]{2,1,0:T(8,128)S(1)}, f32[41,8,128]{2,1,0:T(8,128)S(1)}, u32[]{:S(2)}, u32[]{:S(2)}) %collective-permute-start.7) | collective-permute-done | bytes 167968 | tf_op jit(solution)/shard_map/ppermute | solution.py:369
  58.6 0.0 collective-permute-start.4
  58.6 0.0 copy-done
  58.6 3.0 %shard_map.48 = (f32[4,512,128]{2,1,0:T(8,128)S(1)}, f32[4,512,128]{2,1,0:T(8,128)S(1)}) custom-call(f32[41,8,128]{2,1,0:T(8,128)S(1)} %get-tuple-element.46.refs_0_, f32[41,8,128]{2,1,0:T(8,128)S(1)} %collective-permute-done.13.refs_1_, f32[41,8,128]{2,1,0:T(8,128)S(1)} %collective-permute-done.14.refs_2_, ...), custom_call_target="tpu_custom_call" | custom-call | tf_op jit(solution)/shard_map/pallas_call | solution.py:345
  61.6 1.8 %shard_map.49 = (f32[4,512,128]{2,1,0:T(8,128)S(1)}, f32[4,512,128]{2,1,0:T(8,128)S(1)}) custom-call(f32[41,8,128]{2,1,0:T(8,128)S(1)} %collective-permute-done.11.refs_0_, f32[41,8,128]{2,1,0:T(8,128)S(1)} %collective-permute-done.12.refs_1_, bf16[256,512]{1,0:T(8,128)(2,1)S(1)} %copy-done, ...), custom_call_target="tpu_custom_call", output_to_operand_aliasing={{0}: (3, {}), {1}: (4, {})} | custom-call | tf_op jit(solution)/shard_map/pallas_call | solution.py:345
  63.5 1.8 %shard_map.50 = (f32[4,512,128]{2,1,0:T(8,128)S(1)}, f32[4,512,128]{2,1,0:T(8,128)S(1)}) custom-call(f32[41,8,128]{2,1,0:T(8,128)S(1)} %collective-permute-done.9.refs_0_, f32[41,8,128]{2,1,0:T(8,128)S(1)} %collective-permute-done.10.refs_1_, bf16[256,512]{1,0:T(8,128)(2,1)S(1)} %copy-done, ...), custom_call_target="tpu_custom_call", output_to_operand_aliasing={{0}: (3, {}), {1}: (4, {})} | custom-call | tf_op jit(solution)/shard_map/pallas_call | solution.py:345
  65.3 0.0 collective-permute-done.8.refs_1_
  65.3 1.8 %shard_map.51 = (f32[4,512,128]{2,1,0:T(8,128)S(1)}, f32[4,512,128]{2,1,0:T(8,128)S(1)}) custom-call(f32[41,8,128]{2,1,0:T(8,128)S(1)} %collective-permute-done.7.refs_0_, f32[41,8,128]{2,1,0:T(8,128)S(1)} %collective-permute-done.8.refs_1_, bf16[256,512]{1,0:T(8,128)(2,1)S(1)} %copy-done, ...), custom_call_target="tpu_custom_call", output_to_operand_aliasing={{0}: (3, {}), {1}: (4, {})} | custom-call | tf_op jit(solution)/shard_map/pallas_call | solution.py:345
  67.2 0.0 collective-permute-done.5.refs_0_
  67.2 0.0 collective-permute-done.6.refs_1_
  67.2 1.8 %shard_map.52 = (f32[4,512,128]{2,1,0:T(8,128)S(1)}, f32[4,512,128]{2,1,0:T(8,128)S(1)}) custom-call(f32[41,8,128]{2,1,0:T(8,128)S(1)} %collective-permute-done.5.refs_0_, f32[41,8,128]{2,1,0:T(8,128)S(1)} %collective-permute-done.6.refs_1_, bf16[256,512]{1,0:T(8,128)(2,1)S(1)} %copy-done, ...), custom_call_target="tpu_custom_call", output_to_operand_aliasing={{0}: (3, {}), {1}: (4, {})} | custom-call | tf_op jit(solution)/shard_map/pallas_call | solution.py:345
  69.0 0.0 collective-permute-done.3.refs_0_
  69.0 0.0 collective-permute-done.4.refs_1_
  69.0 1.8 %shard_map.53 = (f32[4,512,128]{2,1,0:T(8,128)S(1)}, f32[4,512,128]{2,1,0:T(8,128)S(1)}) custom-call(f32[41,8,128]{2,1,0:T(8,128)S(1)} %collective-permute-done.3.refs_0_, f32[41,8,128]{2,1,0:T(8,128)S(1)} %collective-permute-done.4.refs_1_, bf16[256,512]{1,0:T(8,128)(2,1)S(1)} %copy-done, ...), custom_call_target="tpu_custom_call", output_to_operand_aliasing={{0}: (3, {}), {1}: (4, {})} | custom-call | tf_op jit(solution)/shard_map/pallas_call | solution.py:345
  70.9 0.1 collective-permute-start.16
  71.0 3.0 %collective-permute-start = (f32[41,8,128]{2,1,0:T(8,128)S(1)}, f32[41,8,128]{2,1,0:T(8,128)S(1)}, u32[]{:S(2)}, u32[]{:S(2)}) collective-permute-start(f32[41,8,128]{2,1,0:T(8,128)S(1)} %get-tuple-element.34), channel_id=1, source_target_pairs={{0,30},{1,31},{2,28},{3,29},{4,26},{5,27},{6,24},{7,25},{8,22},{9,... | collective-permute-start | bytes 503816 | tf_op jit(solution)/shard_map/ppermute | solution.py:369
  74.0 0.0 collective-permute-start.1
  74.0 7.9 %collective-permute-done.refs_0_ = f32[41,8,128]{2,1,0:T(8,128)S(1)} collective-permute-done((f32[41,8,128]{2,1,0:T(8,128)S(1)}, f32[41,8,128]{2,1,0:T(8,128)S(1)}, u32[]{:S(2)}, u32[]{:S(2)}) %collective-permute-start) | collective-permute-done | bytes 167968 | tf_op jit(solution)/shard_map/ppermute | solution.py:369
  81.8 3.1 %collective-permute-done.1.refs_1_ = f32[41,8,128]{2,1,0:T(8,128)S(1)} collective-permute-done((f32[41,8,128]{2,1,0:T(8,128)S(1)}, f32[41,8,128]{2,1,0:T(8,128)S(1)}, u32[]{:S(2)}, u32[]{:S(2)}) %collective-permute-start.1) | collective-permute-done | bytes 167968 | tf_op jit(solution)/shard_map/ppermute | solution.py:369
  85.0 0.1 collective-permute-start.2
  85.1 1.2 %shard_map.54.refs_2_ = f32[4,512,128]{2,1,0:T(8,128)S(1)} custom-call(f32[41,8,128]{2,1,0:T(8,128)S(1)} %collective-permute-done.refs_0_, f32[41,8,128]{2,1,0:T(8,128)S(1)} %collective-permute-done.1.refs_1_, bf16[256,512]{1,0:T(8,128)(2,1)S(1)} %copy-done, f32[4,512,128]{2,1,0:T(8,128)S(1)} %get-tuple-element.60.refs_3_), custom_call_target="tpu_custom_call", output_to_operand_aliasing={{}: (3, {})} | custom-call | tf_op jit(solution)/shard_map/pallas_call | solution.py:345
  86.3 0.2 collective-permute-done.2.refs_0_
  86.5 0.0 collective-permute-done.16.refs_3_
  86.5 2.3 %shard_map.55 = (f32[4,512,128]{2,1,0:T(8,128)}, f32[4,512,128]{2,1,0:T(8,128)S(1)}) custom-call(f32[42,8,128]{2,1,0:T(8,128)S(1)} %collective-permute-done.2.refs_0_, bf16[256,512]{1,0:T(8,128)(2,1)S(1)} %copy-done, f32[4,512,128]{2,1,0:T(8,128)S(1)} %shard_map.54.refs_2_, ...), custom_call_target="tpu_custom_call", output_to_operand_aliasing={{1}: (2, {})} | custom-call | tf_op jit(solution)/shard_map/pallas_call | solution.py:345
  (3 shorter events, 0.0 us)
Async XLA Ops:
  0.0 58.6 %copy-start = (bf16[256,512]{1,0:T(8,128)(2,1)S(1)}, bf16[256,512]{1,0:T(8,128)(2,1)}, u32[]{:S(2)}) copy-start(bf16[256,512]{1,0:T(8,128)(2,1)} %constant.2.clone.refs_4_.refs_2_.refs_1_) | copy-start | bytes 786436
  3.2 11.0 %collective-permute-start.13 = (f32[41,8,128]{2,1,0:T(8,128)S(1)}, f32[41,8,128]{2,1,0:T(8,128)S(1)}, u32[]{:S(2)}, u32[]{:S(2)}) collective-permute-start(f32[41,8,128]{2,1,0:T(8,128)S(1)} %get-tuple-element.47), channel_id=1, source_target_pairs={{0,2},{1,3},{2,0},{3,1},{4,6},{5,7},{6,4},{7,5},{8,10},{9,11},{10,... | collective-permute-start | bytes 503816 | tf_op jit(solution)/shard_map/ppermute | solution.py:369
  6.2 10.6 %collective-permute-start.14 = (f32[41,8,128]{2,1,0:T(8,128)S(1)}, f32[41,8,128]{2,1,0:T(8,128)S(1)}, u32[]{:S(2)}, u32[]{:S(2)}) collective-permute-start(f32[41,8,128]{2,1,0:T(8,128)S(1)} %get-tuple-element.48), channel_id=1, source_target_pairs={{0,4},{1,5},{2,6},{3,7},{4,0},{5,1},{6,2},{7,3},{8,12},{9,13},{10,... | collective-permute-start | bytes 503816 | tf_op jit(solution)/shard_map/ppermute | solution.py:369
  7.7 11.2 %collective-permute-start.15 = (f32[41,8,128]{2,1,0:T(8,128)S(1)}, f32[41,8,128]{2,1,0:T(8,128)S(1)}, u32[]{:S(2)}, u32[]{:S(2)}) collective-permute-start(f32[41,8,128]{2,1,0:T(8,128)S(1)} %get-tuple-element.49), channel_id=1, source_target_pairs={{0,6},{1,7},{2,4},{3,5},{4,2},{5,3},{6,0},{7,1},{8,14},{9,15},{10,... | collective-permute-start | bytes 503816 | tf_op jit(solution)/shard_map/ppermute | solution.py:369
  9.7 25.7 %collective-permute-start.11 = (f32[41,8,128]{2,1,0:T(8,128)S(1)}, f32[41,8,128]{2,1,0:T(8,128)S(1)}, u32[]{:S(2)}, u32[]{:S(2)}) collective-permute-start(f32[41,8,128]{2,1,0:T(8,128)S(1)} %get-tuple-element.44), channel_id=1, source_target_pairs={{0,16},{1,17},{2,18},{3,19},{4,20},{5,21},{6,22},{7,23},{8,24},{9,... | collective-permute-start | bytes 503816 | tf_op jit(solution)/shard_map/ppermute | solution.py:369
  12.8 26.0 %collective-permute-start.12 = (f32[41,8,128]{2,1,0:T(8,128)S(1)}, f32[41,8,128]{2,1,0:T(8,128)S(1)}, u32[]{:S(2)}, u32[]{:S(2)}) collective-permute-start(f32[41,8,128]{2,1,0:T(8,128)S(1)} %get-tuple-element.45), channel_id=1, source_target_pairs={{0,24},{1,25},{2,26},{3,27},{4,28},{5,29},{6,30},{7,31},{8,16},{9,... | collective-permute-start | bytes 503816 | tf_op jit(solution)/shard_map/ppermute | solution.py:369
  14.2 33.1 %collective-permute-start.10 = (f32[41,8,128]{2,1,0:T(8,128)S(1)}, f32[41,8,128]{2,1,0:T(8,128)S(1)}, u32[]{:S(2)}, u32[]{:S(2)}) collective-permute-start(f32[41,8,128]{2,1,0:T(8,128)S(1)} %get-tuple-element.43), channel_id=1, source_target_pairs={{0,20},{1,21},{2,22},{3,23},{4,16},{5,17},{6,18},{7,19},{8,28},{9,... | collective-permute-start | bytes 503816 | tf_op jit(solution)/shard_map/ppermute | solution.py:369
  16.8 33.9 %collective-permute-start.9 = (f32[41,8,128]{2,1,0:T(8,128)S(1)}, f32[41,8,128]{2,1,0:T(8,128)S(1)}, u32[]{:S(2)}, u32[]{:S(2)}) collective-permute-start(f32[41,8,128]{2,1,0:T(8,128)S(1)} %get-tuple-element.42), channel_id=1, source_target_pairs={{0,18},{1,19},{2,16},{3,17},{4,22},{5,23},{6,20},{7,21},{8,26},{9,... | collective-permute-start | bytes 503816 | tf_op jit(solution)/shard_map/ppermute | solution.py:369
  19.0 39.6 %collective-permute-start.7 = (f32[41,8,128]{2,1,0:T(8,128)S(1)}, f32[41,8,128]{2,1,0:T(8,128)S(1)}, u32[]{:S(2)}, u32[]{:S(2)}) collective-permute-start(f32[41,8,128]{2,1,0:T(8,128)S(1)} %get-tuple-element.40), channel_id=1, source_target_pairs={{0,22},{1,23},{2,20},{3,21},{4,18},{5,19},{6,16},{7,17},{8,30},{9,... | collective-permute-start | bytes 503816 | tf_op jit(solution)/shard_map/ppermute | solution.py:369
  35.4 29.9 %collective-permute-start.8 = (f32[41,8,128]{2,1,0:T(8,128)S(1)}, f32[41,8,128]{2,1,0:T(8,128)S(1)}, u32[]{:S(2)}, u32[]{:S(2)}) collective-permute-start(f32[41,8,128]{2,1,0:T(8,128)S(1)} %get-tuple-element.41), channel_id=1, source_target_pairs={{0,26},{1,27},{2,24},{3,25},{4,30},{5,31},{6,28},{7,29},{8,18},{9,... | collective-permute-start | bytes 503816 | tf_op jit(solution)/shard_map/ppermute | solution.py:369
  38.8 28.4 %collective-permute-start.5 = (f32[41,8,128]{2,1,0:T(8,128)S(1)}, f32[41,8,128]{2,1,0:T(8,128)S(1)}, u32[]{:S(2)}, u32[]{:S(2)}) collective-permute-start(f32[41,8,128]{2,1,0:T(8,128)S(1)} %get-tuple-element.38), channel_id=1, source_target_pairs={{0,8},{1,9},{2,10},{3,11},{4,12},{5,13},{6,14},{7,15},{8,0},{9,1},... | collective-permute-start | bytes 503816 | tf_op jit(solution)/shard_map/ppermute | solution.py:369
  47.3 19.9 %collective-permute-start.6 = (f32[41,8,128]{2,1,0:T(8,128)S(1)}, f32[41,8,128]{2,1,0:T(8,128)S(1)}, u32[]{:S(2)}, u32[]{:S(2)}) collective-permute-start(f32[41,8,128]{2,1,0:T(8,128)S(1)} %get-tuple-element.39), channel_id=1, source_target_pairs={{0,10},{1,11},{2,8},{3,9},{4,14},{5,15},{6,12},{7,13},{8,2},{9,3},... | collective-permute-start | bytes 503816 | tf_op jit(solution)/shard_map/ppermute | solution.py:369
  50.7 18.3 %collective-permute-start.3 = (f32[41,8,128]{2,1,0:T(8,128)S(1)}, f32[41,8,128]{2,1,0:T(8,128)S(1)}, u32[]{:S(2)}, u32[]{:S(2)}) collective-permute-start(f32[41,8,128]{2,1,0:T(8,128)S(1)} %get-tuple-element.36), channel_id=1, source_target_pairs={{0,28},{1,29},{2,30},{3,31},{4,24},{5,25},{6,26},{7,27},{8,20},{9,... | collective-permute-start | bytes 503816 | tf_op jit(solution)/shard_map/ppermute | solution.py:369
  58.6 10.5 %collective-permute-start.4 = (f32[41,8,128]{2,1,0:T(8,128)S(1)}, f32[41,8,128]{2,1,0:T(8,128)S(1)}, u32[]{:S(2)}, u32[]{:S(2)}) collective-permute-start(f32[41,8,128]{2,1,0:T(8,128)S(1)} %get-tuple-element.37), channel_id=1, source_target_pairs={{0,12},{1,13},{2,14},{3,15},{4,8},{5,9},{6,10},{7,11},{8,4},{9,5},... | collective-permute-start | bytes 503816 | tf_op jit(solution)/shard_map/ppermute | solution.py:369
  70.9 15.6 %collective-permute-start.16 = (f32[4,512,128]{2,1,0:T(8,128)S(1)}, f32[4,512,128]{2,1,0:T(8,128)S(1)}, u32[]{:S(2)}, u32[]{:S(2)}) collective-permute-start(f32[4,512,128]{2,1,0:T(8,128)S(1)} %get-tuple-element.61), channel_id=1, source_target_pairs={{0,1},{1,0},{2,3},{3,2},{4,5},{5,4},{6,7},{7,6},{8,9},{9,8},{10,11... | collective-permute-start | bytes 3145736 | tf_op jit(solution)/shard_map/ppermute | solution.py:369
  71.0 10.9 %collective-permute-start = (f32[41,8,128]{2,1,0:T(8,128)S(1)}, f32[41,8,128]{2,1,0:T(8,128)S(1)}, u32[]{:S(2)}, u32[]{:S(2)}) collective-permute-start(f32[41,8,128]{2,1,0:T(8,128)S(1)} %get-tuple-element.34), channel_id=1, source_target_pairs={{0,30},{1,31},{2,28},{3,29},{4,26},{5,27},{6,24},{7,25},{8,22},{9,... | collective-permute-start | bytes 503816 | tf_op jit(solution)/shard_map/ppermute | solution.py:369
  74.0 11.0 %collective-permute-start.1 = (f32[41,8,128]{2,1,0:T(8,128)S(1)}, f32[41,8,128]{2,1,0:T(8,128)S(1)}, u32[]{:S(2)}, u32[]{:S(2)}) collective-permute-start(f32[41,8,128]{2,1,0:T(8,128)S(1)} %get-tuple-element.35), channel_id=1, source_target_pairs={{0,14},{1,15},{2,12},{3,13},{4,10},{5,11},{6,8},{7,9},{8,6},{9,7},... | collective-permute-start | bytes 503816 | tf_op jit(solution)/shard_map/ppermute | solution.py:369
  85.0 1.5 %collective-permute-start.2 = (f32[42,8,128]{2,1,0:T(8,128)S(1)}, f32[42,8,128]{2,1,0:T(8,128)S(1)}, u32[]{:S(2)}, u32[]{:S(2)}) collective-permute-start(f32[42,8,128]{2,1,0:T(8,128)S(1)} %pad_maximum_fusion), channel_id=1, source_target_pairs={{0,1},{1,0},{2,3},{3,2},{4,5},{5,4},{6,7},{7,6},{8,9},{9,8},{10,11... | collective-permute-start | bytes 516104 | tf_op jit(solution)/shard_map/ppermute | solution.py:369

commit v4 on v3

--- a/solution.py
+++ b/solution.py
@@ -142,18 +142,32 @@
     ]
     for head in heads:
         head.start()
+    r, t = lax.axis_index("src"), lax.axis_index("tile")
+    offsets = sorted({dt ^ side for _, dt in sends for side in range(2)})
+    ahead = buf.shape[0] == len(offsets) * group
+    copies = []
+    if ahead:
+        for n, offset in enumerate(offsets):
+            for i in range(group):
+                s = n * group + i
+                copy = pltpu.make_async_copy(
+                    tables_ref.at[(t ^ offset) * group + i], buf.at[s], sem.at[s]
+                )
+                copy.start()
+                copies.append(copy)
     for head in heads:
         head.wait()
-    r, t = lax.axis_index("src"), lax.axis_index("tile")
     lanes = lax.broadcasted_iota(jnp.int32, (SUB, LANES), 1)
-    offsets = sorted({dt ^ side for _, dt in sends for side in range(2)})
-    found, copies = {}, []
+    found = {}
     for n, offset in enumerate(offsets):
         g = t ^ offset
         for j in range(SLOTS):
             local, weight = slot_scalars(mask_ref, weight_ref, g * group, group, j)
-            found[offset, j] = (n * SLOTS + j, local, weight)
+            if ahead:
+                found[offset, j] = (n * group + local, local, weight)
+                continue
             s = n * SLOTS + j
+            found[offset, j] = (s, local, weight)
             copy = pltpu.make_async_copy(tables_ref.at[g * group + local], buf.at[s], sem.at[s])
             copy.start()
             copies.append(copy)
@@ -189,7 +203,8 @@
 def pick(sends, bricks, weights, aperture, owners):
     group = bricks.shape[0] // owners
     quarters = bricks.shape[1]
-    slots = SLOTS * len({dt ^ side for _, dt in sends for side in range(2)})
+    needed = len({dt ^ side for _, dt in sends for side in range(2)})
+    slots = needed * (group if needed == 2 else SLOTS)
     home = functools.partial(pltpu.with_memory_space_constraint, memory_space=pltpu.HBM)
     return pl.pallas_call(
         functools.partial(pick_kernel, sends, quarters, group),

time: 88.9 us -> 88.4 us (level)
  no operation moved by 1% of the time
where the time goes in v4:
time: 88.4 us; the launch traced here: 88.2 us
  waiting for transfers between devices  39.4 us (45%)
  starting transfers between devices  28.4 us (32%)
  Pallas kernels  20.3 us (23%)
    ppermute x17, waiting for transfers between devices, permute(): return lax.ppermute(value, ('src', 'tile'), pairs)  39.4 us
    ppermute x17, starting transfers between devices, permute(): return lax.ppermute(value, ('src', 'tile'), pairs)  28.4 us
    pallas_call x8, Pallas kernels, image_step(): pl.pallas_call(functools.partial(image_kernel, entries, rows, len(arrays)...  15.7 us
    pallas_call x2, Pallas kernels, pick(): pl.pallas_call(functools.partial(pick_kernel, sends, quarters, group), ou...  4.62 us
  transfers between devices with their start and end apart: 17, of which 7 were waited for; matrix products, arithmetic and copies ran while one was open for 0% of the time, Pallas kernels for 15%

profile of v4, /device:TPU:0, one launch (start us, length us, event | category | flops | bytes accessed | tf_op | source)
XLA Modules:
  0.0 88.2 jit_solution(5526817461299256208)
XLA Ops:
  0.0 0.0 copy-start
  0.0 3.2 %shard_map.46 = (f32[41,8,128]{2,1,0:T(8,128)S(1)}, f32[41,8,128]{2,1,0:T(8,128)S(1)}, f32[41,8,128]{2,1,0:T(8,128)S(1)}, f32[41,8,128]{2,1,0:T(8,128)S(1)}, f32...) custom-call(s32[1,32]{1,0:T(1,128)} %mask_in.3, ...), custom_call_target="tpu_custom_call" | custom-call | tf_op jit(solution)/shard_map/pallas_call | solution.py:209
  3.2 3.0 %collective-permute-start.13 = (f32[41,8,128]{2,1,0:T(8,128)S(1)}, f32[41,8,128]{2,1,0:T(8,128)S(1)}, u32[]{:S(2)}, u32[]{:S(2)}) collective-permute-start(f32[41,8,128]{2,1,0:T(8,128)S(1)} %get-tuple-element.47), channel_id=1, source_target_pairs={{0,2},{1,3},{2,0},{3,1},{4,6},{5,7},{6,4},{7,5},{8,10},{9,11},{10,... | collective-permute-start | bytes 503816 | tf_op jit(solution)/shard_map/ppermute | solution.py:384
  6.2 1.5 %collective-permute-start.14 = (f32[41,8,128]{2,1,0:T(8,128)S(1)}, f32[41,8,128]{2,1,0:T(8,128)S(1)}, u32[]{:S(2)}, u32[]{:S(2)}) collective-permute-start(f32[41,8,128]{2,1,0:T(8,128)S(1)} %get-tuple-element.48), channel_id=1, source_target_pairs={{0,4},{1,5},{2,6},{3,7},{4,0},{5,1},{6,2},{7,3},{8,12},{9,13},{10,... | collective-permute-start | bytes 503816 | tf_op jit(solution)/shard_map/ppermute | solution.py:384
  7.7 0.0 collective-permute-start.15
  7.7 1.5 %shard_map.47 = (f32[41,8,128]{2,1,0:T(8,128)S(1)}, f32[41,8,128]{2,1,0:T(8,128)S(1)}) custom-call(s32[1,32]{1,0:T(1,128)} %mask_in.3, f32[1,32]{1,0:T(1,128)} %weight_in.3, f32[32,4,8,1024]{3,2,1,0:T(8,128)} %bitcast.3), custom_call_target="tpu_custom_call" | custom-call | tf_op jit(solution)/shard_map/pallas_call | solution.py:209
  9.2 3.1 %collective-permute-start.11 = (f32[41,8,128]{2,1,0:T(8,128)S(1)}, f32[41,8,128]{2,1,0:T(8,128)S(1)}, u32[]{:S(2)}, u32[]{:S(2)}) collective-permute-start(f32[41,8,128]{2,1,0:T(8,128)S(1)} %get-tuple-element.44), channel_id=1, source_target_pairs={{0,16},{1,17},{2,18},{3,19},{4,20},{5,21},{6,22},{7,23},{8,24},{9,... | collective-permute-start | bytes 503816 | tf_op jit(solution)/shard_map/ppermute | solution.py:384
  12.3 1.3 %collective-permute-start.12 = (f32[41,8,128]{2,1,0:T(8,128)S(1)}, f32[41,8,128]{2,1,0:T(8,128)S(1)}, u32[]{:S(2)}, u32[]{:S(2)}) collective-permute-start(f32[41,8,128]{2,1,0:T(8,128)S(1)} %get-tuple-element.45), channel_id=1, source_target_pairs={{0,24},{1,25},{2,26},{3,27},{4,28},{5,29},{6,30},{7,31},{8,16},{9,... | collective-permute-start | bytes 503816 | tf_op jit(solution)/shard_map/ppermute | solution.py:384
  13.7 0.0 collective-permute-done.13.refs_1_
  13.7 2.6 %collective-permute-start.10 = (f32[41,8,128]{2,1,0:T(8,128)S(1)}, f32[41,8,128]{2,1,0:T(8,128)S(1)}, u32[]{:S(2)}, u32[]{:S(2)}) collective-permute-start(f32[41,8,128]{2,1,0:T(8,128)S(1)} %get-tuple-element.43), channel_id=1, source_target_pairs={{0,20},{1,21},{2,22},{3,23},{4,16},{5,17},{6,18},{7,19},{8,28},{9,... | collective-permute-start | bytes 503816 | tf_op jit(solution)/shard_map/ppermute | solution.py:384
  16.3 0.0 collective-permute-done.14.refs_2_
  16.3 2.2 %collective-permute-start.9 = (f32[41,8,128]{2,1,0:T(8,128)S(1)}, f32[41,8,128]{2,1,0:T(8,128)S(1)}, u32[]{:S(2)}, u32[]{:S(2)}) collective-permute-start(f32[41,8,128]{2,1,0:T(8,128)S(1)} %get-tuple-element.42), channel_id=1, source_target_pairs={{0,18},{1,19},{2,16},{3,17},{4,22},{5,23},{6,20},{7,21},{8,26},{9,... | collective-permute-start | bytes 503816 | tf_op jit(solution)/shard_map/ppermute | solution.py:384
  18.5 0.0 collective-permute-done.15.refs_3_
  18.5 1.8 %collective-permute-start.7 = (f32[41,8,128]{2,1,0:T(8,128)S(1)}, f32[41,8,128]{2,1,0:T(8,128)S(1)}, u32[]{:S(2)}, u32[]{:S(2)}) collective-permute-start(f32[41,8,128]{2,1,0:T(8,128)S(1)} %get-tuple-element.40), channel_id=1, source_target_pairs={{0,22},{1,23},{2,20},{3,21},{4,18},{5,19},{6,16},{7,17},{8,30},{9,... | collective-permute-start | bytes 503816 | tf_op jit(solution)/shard_map/ppermute | solution.py:384
  20.3 14.6 %collective-permute-done.11.refs_0_ = f32[41,8,128]{2,1,0:T(8,128)S(1)} collective-permute-done((f32[41,8,128]{2,1,0:T(8,128)S(1)}, f32[41,8,128]{2,1,0:T(8,128)S(1)}, u32[]{:S(2)}, u32[]{:S(2)}) %collective-permute-start.11) | collective-permute-done | bytes 167968 | tf_op jit(solution)/shard_map/ppermute | solution.py:384
  34.9 3.4 %collective-permute-start.8 = (f32[41,8,128]{2,1,0:T(8,128)S(1)}, f32[41,8,128]{2,1,0:T(8,128)S(1)}, u32[]{:S(2)}, u32[]{:S(2)}) collective-permute-start(f32[41,8,128]{2,1,0:T(8,128)S(1)} %get-tuple-element.41), channel_id=1, source_target_pairs={{0,26},{1,27},{2,24},{3,25},{4,30},{5,31},{6,28},{7,29},{8,18},{9,... | collective-permute-start | bytes 503816 | tf_op jit(solution)/shard_map/ppermute | solution.py:384
  38.3 0.0 collective-permute-done.12.refs_1_
  38.3 2.6 %collective-permute-start.5 = (f32[41,8,128]{2,1,0:T(8,128)S(1)}, f32[41,8,128]{2,1,0:T(8,128)S(1)}, u32[]{:S(2)}, u32[]{:S(2)}) collective-permute-start(f32[41,8,128]{2,1,0:T(8,128)S(1)} %get-tuple-element.38), channel_id=1, source_target_pairs={{0,8},{1,9},{2,10},{3,11},{4,12},{5,13},{6,14},{7,15},{8,0},{9,1},... | collective-permute-start | bytes 503816 | tf_op jit(solution)/shard_map/ppermute | solution.py:384
  40.9 5.9 %collective-permute-done.10.refs_1_ = f32[41,8,128]{2,1,0:T(8,128)S(1)} collective-permute-done((f32[41,8,128]{2,1,0:T(8,128)S(1)}, f32[41,8,128]{2,1,0:T(8,128)S(1)}, u32[]{:S(2)}, u32[]{:S(2)}) %collective-permute-start.10) | collective-permute-done | bytes 167968 | tf_op jit(solution)/shard_map/ppermute | solution.py:384
  46.8 0.0 collective-permute-start.6
  46.8 3.5 %collective-permute-done.9.refs_0_ = f32[41,8,128]{2,1,0:T(8,128)S(1)} collective-permute-done((f32[41,8,128]{2,1,0:T(8,128)S(1)}, f32[41,8,128]{2,1,0:T(8,128)S(1)}, u32[]{:S(2)}, u32[]{:S(2)}) %collective-permute-start.9) | collective-permute-done | bytes 167968 | tf_op jit(solution)/shard_map/ppermute | solution.py:384
  50.2 3.5 %collective-permute-start.3 = (f32[41,8,128]{2,1,0:T(8,128)S(1)}, f32[41,8,128]{2,1,0:T(8,128)S(1)}, u32[]{:S(2)}, u32[]{:S(2)}) collective-permute-start(f32[41,8,128]{2,1,0:T(8,128)S(1)} %get-tuple-element.36), channel_id=1, source_target_pairs={{0,28},{1,29},{2,30},{3,31},{4,24},{5,25},{6,26},{7,27},{8,20},{9,... | collective-permute-start | bytes 503816 | tf_op jit(solution)/shard_map/ppermute | solution.py:384
  53.8 4.3 %collective-permute-done.7.refs_0_ = f32[41,8,128]{2,1,0:T(8,128)S(1)} collective-permute-done((f32[41,8,128]{2,1,0:T(8,128)S(1)}, f32[41,8,128]{2,1,0:T(8,128)S(1)}, u32[]{:S(2)}, u32[]{:S(2)}) %collective-permute-start.7) | collective-permute-done | bytes 167968 | tf_op jit(solution)/shard_map/ppermute | solution.py:384
  58.1 0.0 collective-permute-start.4
  58.1 0.0 copy-done
  58.1 3.0 %shard_map.48 = (f32[4,512,128]{2,1,0:T(8,128)S(1)}, f32[4,512,128]{2,1,0:T(8,128)S(1)}) custom-call(f32[41,8,128]{2,1,0:T(8,128)S(1)} %get-tuple-element.46.refs_0_, f32[41,8,128]{2,1,0:T(8,128)S(1)} %collective-permute-done.13.refs_1_, f32[41,8,128]{2,1,0:T(8,128)S(1)} %collective-permute-done.14.refs_2_, ...), custom_call_target="tpu_custom_call" | custom-call | tf_op jit(solution)/shard_map/pallas_call | solution.py:360
  61.1 1.8 %shard_map.49 = (f32[4,512,128]{2,1,0:T(8,128)S(1)}, f32[4,512,128]{2,1,0:T(8,128)S(1)}) custom-call(f32[41,8,128]{2,1,0:T(8,128)S(1)} %collective-permute-done.11.refs_0_, f32[41,8,128]{2,1,0:T(8,128)S(1)} %collective-permute-done.12.refs_1_, bf16[256,512]{1,0:T(8,128)(2,1)S(1)} %copy-done, ...), custom_call_target="tpu_custom_call", output_to_operand_aliasing={{0}: (3, {}), {1}: (4, {})} | custom-call | tf_op jit(solution)/shard_map/pallas_call | solution.py:360
  63.0 1.8 %shard_map.50 = (f32[4,512,128]{2,1,0:T(8,128)S(1)}, f32[4,512,128]{2,1,0:T(8,128)S(1)}) custom-call(f32[41,8,128]{2,1,0:T(8,128)S(1)} %collective-permute-done.9.refs_0_, f32[41,8,128]{2,1,0:T(8,128)S(1)} %collective-permute-done.10.refs_1_, bf16[256,512]{1,0:T(8,128)(2,1)S(1)} %copy-done, ...), custom_call_target="tpu_custom_call", output_to_operand_aliasing={{0}: (3, {}), {1}: (4, {})} | custom-call | tf_op jit(solution)/shard_map/pallas_call | solution.py:360
  64.8 0.0 collective-permute-done.8.refs_1_
  64.8 1.8 %shard_map.51 = (f32[4,512,128]{2,1,0:T(8,128)S(1)}, f32[4,512,128]{2,1,0:T(8,128)S(1)}) custom-call(f32[41,8,128]{2,1,0:T(8,128)S(1)} %collective-permute-done.7.refs_0_, f32[41,8,128]{2,1,0:T(8,128)S(1)} %collective-permute-done.8.refs_1_, bf16[256,512]{1,0:T(8,128)(2,1)S(1)} %copy-done, ...), custom_call_target="tpu_custom_call", output_to_operand_aliasing={{0}: (3, {}), {1}: (4, {})} | custom-call | tf_op jit(solution)/shard_map/pallas_call | solution.py:360
  66.7 0.0 collective-permute-done.5.refs_0_
  66.7 0.0 collective-permute-done.6.refs_1_
  66.7 1.8 %shard_map.52 = (f32[4,512,128]{2,1,0:T(8,128)S(1)}, f32[4,512,128]{2,1,0:T(8,128)S(1)}) custom-call(f32[41,8,128]{2,1,0:T(8,128)S(1)} %collective-permute-done.5.refs_0_, f32[41,8,128]{2,1,0:T(8,128)S(1)} %collective-permute-done.6.refs_1_, bf16[256,512]{1,0:T(8,128)(2,1)S(1)} %copy-done, ...), custom_call_target="tpu_custom_call", output_to_operand_aliasing={{0}: (3, {}), {1}: (4, {})} | custom-call | tf_op jit(solution)/shard_map/pallas_call | solution.py:360
  68.5 0.0 collective-permute-done.3.refs_0_
  68.5 0.0 collective-permute-done.4.refs_1_
  68.6 1.8 %shard_map.53 = (f32[4,512,128]{2,1,0:T(8,128)S(1)}, f32[4,512,128]{2,1,0:T(8,128)S(1)}) custom-call(f32[41,8,128]{2,1,0:T(8,128)S(1)} %collective-permute-done.3.refs_0_, f32[41,8,128]{2,1,0:T(8,128)S(1)} %collective-permute-done.4.refs_1_, bf16[256,512]{1,0:T(8,128)(2,1)S(1)} %copy-done, ...), custom_call_target="tpu_custom_call", output_to_operand_aliasing={{0}: (3, {}), {1}: (4, {})} | custom-call | tf_op jit(solution)/shard_map/pallas_call | solution.py:360
  70.4 0.1 collective-permute-start.16
  70.5 3.0 %collective-permute-start = (f32[41,8,128]{2,1,0:T(8,128)S(1)}, f32[41,8,128]{2,1,0:T(8,128)S(1)}, u32[]{:S(2)}, u32[]{:S(2)}) collective-permute-start(f32[41,8,128]{2,1,0:T(8,128)S(1)} %get-tuple-element.34), channel_id=1, source_target_pairs={{0,30},{1,31},{2,28},{3,29},{4,26},{5,27},{6,24},{7,25},{8,22},{9,... | collective-permute-start | bytes 503816 | tf_op jit(solution)/shard_map/ppermute | solution.py:384
  73.5 0.0 collective-permute-start.1
  73.5 7.8 %collective-permute-done.refs_0_ = f32[41,8,128]{2,1,0:T(8,128)S(1)} collective-permute-done((f32[41,8,128]{2,1,0:T(8,128)S(1)}, f32[41,8,128]{2,1,0:T(8,128)S(1)}, u32[]{:S(2)}, u32[]{:S(2)}) %collective-permute-start) | collective-permute-done | bytes 167968 | tf_op jit(solution)/shard_map/ppermute | solution.py:384
  81.4 3.1 %collective-permute-done.1.refs_1_ = f32[41,8,128]{2,1,0:T(8,128)S(1)} collective-permute-done((f32[41,8,128]{2,1,0:T(8,128)S(1)}, f32[41,8,128]{2,1,0:T(8,128)S(1)}, u32[]{:S(2)}, u32[]{:S(2)}) %collective-permute-start.1) | collective-permute-done | bytes 167968 | tf_op jit(solution)/shard_map/ppermute | solution.py:384
  84.5 0.1 collective-permute-start.2
  84.6 1.2 %shard_map.54.refs_2_ = f32[4,512,128]{2,1,0:T(8,128)S(1)} custom-call(f32[41,8,128]{2,1,0:T(8,128)S(1)} %collective-permute-done.refs_0_, f32[41,8,128]{2,1,0:T(8,128)S(1)} %collective-permute-done.1.refs_1_, bf16[256,512]{1,0:T(8,128)(2,1)S(1)} %copy-done, f32[4,512,128]{2,1,0:T(8,128)S(1)} %get-tuple-element.60.refs_3_), custom_call_target="tpu_custom_call", output_to_operand_aliasing={{}: (3, {})} | custom-call | tf_op jit(solution)/shard_map/pallas_call | solution.py:360
  85.8 0.2 collective-permute-done.2.refs_0_
  86.0 0.0 collective-permute-done.16.refs_3_
  86.0 2.3 %shard_map.55 = (f32[4,512,128]{2,1,0:T(8,128)}, f32[4,512,128]{2,1,0:T(8,128)S(1)}) custom-call(f32[42,8,128]{2,1,0:T(8,128)S(1)} %collective-permute-done.2.refs_0_, bf16[256,512]{1,0:T(8,128)(2,1)S(1)} %copy-done, f32[4,512,128]{2,1,0:T(8,128)S(1)} %shard_map.54.refs_2_, ...), custom_call_target="tpu_custom_call", output_to_operand_aliasing={{1}: (2, {})} | custom-call | tf_op jit(solution)/shard_map/pallas_call | solution.py:360
  (3 shorter events, 0.0 us)
Async XLA Ops:
  0.0 58.1 %copy-start = (bf16[256,512]{1,0:T(8,128)(2,1)S(1)}, bf16[256,512]{1,0:T(8,128)(2,1)}, u32[]{:S(2)}) copy-start(bf16[256,512]{1,0:T(8,128)(2,1)} %constant.2.clone.refs_4_.refs_2_.refs_1_) | copy-start | bytes 786436
  3.2 10.5 %collective-permute-start.13 = (f32[41,8,128]{2,1,0:T(8,128)S(1)}, f32[41,8,128]{2,1,0:T(8,128)S(1)}, u32[]{:S(2)}, u32[]{:S(2)}) collective-permute-start(f32[41,8,128]{2,1,0:T(8,128)S(1)} %get-tuple-element.47), channel_id=1, source_target_pairs={{0,2},{1,3},{2,0},{3,1},{4,6},{5,7},{6,4},{7,5},{8,10},{9,11},{10,... | collective-permute-start | bytes 503816 | tf_op jit(solution)/shard_map/ppermute | solution.py:384
  6.2 10.1 %collective-permute-start.14 = (f32[41,8,128]{2,1,0:T(8,128)S(1)}, f32[41,8,128]{2,1,0:T(8,128)S(1)}, u32[]{:S(2)}, u32[]{:S(2)}) collective-permute-start(f32[41,8,128]{2,1,0:T(8,128)S(1)} %get-tuple-element.48), channel_id=1, source_target_pairs={{0,4},{1,5},{2,6},{3,7},{4,0},{5,1},{6,2},{7,3},{8,12},{9,13},{10,... | collective-permute-start | bytes 503816 | tf_op jit(solution)/shard_map/ppermute | solution.py:384
  7.7 10.8 %collective-permute-start.15 = (f32[41,8,128]{2,1,0:T(8,128)S(1)}, f32[41,8,128]{2,1,0:T(8,128)S(1)}, u32[]{:S(2)}, u32[]{:S(2)}) collective-permute-start(f32[41,8,128]{2,1,0:T(8,128)S(1)} %get-tuple-element.49), channel_id=1, source_target_pairs={{0,6},{1,7},{2,4},{3,5},{4,2},{5,3},{6,0},{7,1},{8,14},{9,15},{10,... | collective-permute-start | bytes 503816 | tf_op jit(solution)/shard_map/ppermute | solution.py:384
  9.2 25.7 %collective-permute-start.11 = (f32[41,8,128]{2,1,0:T(8,128)S(1)}, f32[41,8,128]{2,1,0:T(8,128)S(1)}, u32[]{:S(2)}, u32[]{:S(2)}) collective-permute-start(f32[41,8,128]{2,1,0:T(8,128)S(1)} %get-tuple-element.44), channel_id=1, source_target_pairs={{0,16},{1,17},{2,18},{3,19},{4,20},{5,21},{6,22},{7,23},{8,24},{9,... | collective-permute-start | bytes 503816 | tf_op jit(solution)/shard_map/ppermute | solution.py:384
  12.3 26.0 %collective-permute-start.12 = (f32[41,8,128]{2,1,0:T(8,128)S(1)}, f32[41,8,128]{2,1,0:T(8,128)S(1)}, u32[]{:S(2)}, u32[]{:S(2)}) collective-permute-start(f32[41,8,128]{2,1,0:T(8,128)S(1)} %get-tuple-element.45), channel_id=1, source_target_pairs={{0,24},{1,25},{2,26},{3,27},{4,28},{5,29},{6,30},{7,31},{8,16},{9,... | collective-permute-start | bytes 503816 | tf_op jit(solution)/shard_map/ppermute | solution.py:384
  13.7 33.1 %collective-permute-start.10 = (f32[41,8,128]{2,1,0:T(8,128)S(1)}, f32[41,8,128]{2,1,0:T(8,128)S(1)}, u32[]{:S(2)}, u32[]{:S(2)}) collective-permute-start(f32[41,8,128]{2,1,0:T(8,128)S(1)} %get-tuple-element.43), channel_id=1, source_target_pairs={{0,20},{1,21},{2,22},{3,23},{4,16},{5,17},{6,18},{7,19},{8,28},{9,... | collective-permute-start | bytes 503816 | tf_op jit(solution)/shard_map/ppermute | solution.py:384
  16.3 33.9 %collective-permute-start.9 = (f32[41,8,128]{2,1,0:T(8,128)S(1)}, f32[41,8,128]{2,1,0:T(8,128)S(1)}, u32[]{:S(2)}, u32[]{:S(2)}) collective-permute-start(f32[41,8,128]{2,1,0:T(8,128)S(1)} %get-tuple-element.42), channel_id=1, source_target_pairs={{0,18},{1,19},{2,16},{3,17},{4,22},{5,23},{6,20},{7,21},{8,26},{9,... | collective-permute-start | bytes 503816 | tf_op jit(solution)/shard_map/ppermute | solution.py:384
  18.5 39.6 %collective-permute-start.7 = (f32[41,8,128]{2,1,0:T(8,128)S(1)}, f32[41,8,128]{2,1,0:T(8,128)S(1)}, u32[]{:S(2)}, u32[]{:S(2)}) collective-permute-start(f32[41,8,128]{2,1,0:T(8,128)S(1)} %get-tuple-element.40), channel_id=1, source_target_pairs={{0,22},{1,23},{2,20},{3,21},{4,18},{5,19},{6,16},{7,17},{8,30},{9,... | collective-permute-start | bytes 503816 | tf_op jit(solution)/shard_map/ppermute | solution.py:384
  34.9 29.9 %collective-permute-start.8 = (f32[41,8,128]{2,1,0:T(8,128)S(1)}, f32[41,8,128]{2,1,0:T(8,128)S(1)}, u32[]{:S(2)}, u32[]{:S(2)}) collective-permute-start(f32[41,8,128]{2,1,0:T(8,128)S(1)} %get-tuple-element.41), channel_id=1, source_target_pairs={{0,26},{1,27},{2,24},{3,25},{4,30},{5,31},{6,28},{7,29},{8,18},{9,... | collective-permute-start | bytes 503816 | tf_op jit(solution)/shard_map/ppermute | solution.py:384
  38.3 28.4 %collective-permute-start.5 = (f32[41,8,128]{2,1,0:T(8,128)S(1)}, f32[41,8,128]{2,1,0:T(8,128)S(1)}, u32[]{:S(2)}, u32[]{:S(2)}) collective-permute-start(f32[41,8,128]{2,1,0:T(8,128)S(1)} %get-tuple-element.38), channel_id=1, source_target_pairs={{0,8},{1,9},{2,10},{3,11},{4,12},{5,13},{6,14},{7,15},{8,0},{9,1},... | collective-permute-start | bytes 503816 | tf_op jit(solution)/shard_map/ppermute | solution.py:384
  46.8 19.9 %collective-permute-start.6 = (f32[41,8,128]{2,1,0:T(8,128)S(1)}, f32[41,8,128]{2,1,0:T(8,128)S(1)}, u32[]{:S(2)}, u32[]{:S(2)}) collective-permute-start(f32[41,8,128]{2,1,0:T(8,128)S(1)} %get-tuple-element.39), channel_id=1, source_target_pairs={{0,10},{1,11},{2,8},{3,9},{4,14},{5,15},{6,12},{7,13},{8,2},{9,3},... | collective-permute-start | bytes 503816 | tf_op jit(solution)/shard_map/ppermute | solution.py:384
  50.2 18.3 %collective-permute-start.3 = (f32[41,8,128]{2,1,0:T(8,128)S(1)}, f32[41,8,128]{2,1,0:T(8,128)S(1)}, u32[]{:S(2)}, u32[]{:S(2)}) collective-permute-start(f32[41,8,128]{2,1,0:T(8,128)S(1)} %get-tuple-element.36), channel_id=1, source_target_pairs={{0,28},{1,29},{2,30},{3,31},{4,24},{5,25},{6,26},{7,27},{8,20},{9,... | collective-permute-start | bytes 503816 | tf_op jit(solution)/shard_map/ppermute | solution.py:384
  58.1 10.5 %collective-permute-start.4 = (f32[41,8,128]{2,1,0:T(8,128)S(1)}, f32[41,8,128]{2,1,0:T(8,128)S(1)}, u32[]{:S(2)}, u32[]{:S(2)}) collective-permute-start(f32[41,8,128]{2,1,0:T(8,128)S(1)} %get-tuple-element.37), channel_id=1, source_target_pairs={{0,12},{1,13},{2,14},{3,15},{4,8},{5,9},{6,10},{7,11},{8,4},{9,5},... | collective-permute-start | bytes 503816 | tf_op jit(solution)/shard_map/ppermute | solution.py:384
  70.4 15.6 %collective-permute-start.16 = (f32[4,512,128]{2,1,0:T(8,128)S(1)}, f32[4,512,128]{2,1,0:T(8,128)S(1)}, u32[]{:S(2)}, u32[]{:S(2)}) collective-permute-start(f32[4,512,128]{2,1,0:T(8,128)S(1)} %get-tuple-element.61), channel_id=1, source_target_pairs={{0,1},{1,0},{2,3},{3,2},{4,5},{5,4},{6,7},{7,6},{8,9},{9,8},{10,11... | collective-permute-start | bytes 3145736 | tf_op jit(solution)/shard_map/ppermute | solution.py:384
  70.5 10.9 %collective-permute-start = (f32[41,8,128]{2,1,0:T(8,128)S(1)}, f32[41,8,128]{2,1,0:T(8,128)S(1)}, u32[]{:S(2)}, u32[]{:S(2)}) collective-permute-start(f32[41,8,128]{2,1,0:T(8,128)S(1)} %get-tuple-element.34), channel_id=1, source_target_pairs={{0,30},{1,31},{2,28},{3,29},{4,26},{5,27},{6,24},{7,25},{8,22},{9,... | collective-permute-start | bytes 503816 | tf_op jit(solution)/shard_map/ppermute | solution.py:384
  73.5 11.0 %collective-permute-start.1 = (f32[41,8,128]{2,1,0:T(8,128)S(1)}, f32[41,8,128]{2,1,0:T(8,128)S(1)}, u32[]{:S(2)}, u32[]{:S(2)}) collective-permute-start(f32[41,8,128]{2,1,0:T(8,128)S(1)} %get-tuple-element.35), channel_id=1, source_target_pairs={{0,14},{1,15},{2,12},{3,13},{4,10},{5,11},{6,8},{7,9},{8,6},{9,7},... | collective-permute-start | bytes 503816 | tf_op jit(solution)/shard_map/ppermute | solution.py:384
  84.5 1.5 %collective-permute-start.2 = (f32[42,8,128]{2,1,0:T(8,128)S(1)}, f32[42,8,128]{2,1,0:T(8,128)S(1)}, u32[]{:S(2)}, u32[]{:S(2)}) collective-permute-start(f32[42,8,128]{2,1,0:T(8,128)S(1)} %pad_maximum_fusion), channel_id=1, source_target_pairs={{0,1},{1,0},{2,3},{3,2},{4,5},{5,4},{6,7},{7,6},{8,9},{9,8},{10,11... | collective-permute-start | bytes 516104 | tf_op jit(solution)/shard_map/ppermute | solution.py:384

commit v5 on v4

--- a/solution.py
+++ b/solution.py
@@ -173,7 +173,7 @@
             copies.append(copy)
     for out_ref, (dz, dt) in zip(outs, sends):
         info = jnp.zeros((SUB, LANES), jnp.float32)
-        for side in range(2):
+        for side in range(1 if out_ref.shape[0] <= SIDE + 1 else 2):
             for j in range(SLOTS):
                 _, local, weight = found[dt ^ side, j]
                 lane = 2 * (side * SLOTS + j)
@@ -185,7 +185,7 @@
     for out_ref, (dz, dt) in zip(outs, sends):
         q = r ^ dz
         below, above = jnp.maximum(q - 1, 0), jnp.minimum(q + 1, quarters - 1)
-        for side in range(2):
+        for side in range(1 if out_ref.shape[0] <= SIDE + 1 else 2):
             for j in range(SLOTS):
                 s = found[dt ^ side, j][0]
                 first = side * (SIDE + 1) + j * BLOCK
@@ -200,7 +200,7 @@
                     )
 
 
-def pick(sends, bricks, weights, aperture, owners):
+def pick(sends, single, bricks, weights, aperture, owners):
     group = bricks.shape[0] // owners
     quarters = bricks.shape[1]
     needed = len({dt ^ side for _, dt in sends for side in range(2)})
@@ -208,7 +208,10 @@
     home = functools.partial(pltpu.with_memory_space_constraint, memory_space=pltpu.HBM)
     return pl.pallas_call(
         functools.partial(pick_kernel, sends, quarters, group),
-        out_shape=[pltpu.VMEM((MESSAGE, SUB, LANES), jnp.float32) for _ in sends],
+        out_shape=[
+            pltpu.VMEM((SIDE + 1 if key in single else MESSAGE, SUB, LANES), jnp.float32)
+            for key in sends
+        ],
         in_specs=[pl.BlockSpec(memory_space=pltpu.HBM)] * 3,
         out_specs=[pl.BlockSpec(memory_space=pltpu.VMEM) for _ in sends],
         scratch_shapes=[
@@ -386,22 +389,17 @@
     chips = range(0, owners, 2)
     lead = [(2, 0), (3, 0)]
     near = [(0, dt) for dt in chips[1:]]
-    far = [(dz, dt) for dz in (2, 3) for dt in chips[1:]]
-    side = [(1, dt) for dt in chips]
+    late = [(3, 4), (3, 5), (1, 6), (1, 7)]
+    last = [[(3, 6), (3, 7)], [(1, 4), (1, 5)]]
+    single = set(late + last[0] + last[1])
+    far = [(2, 2), (2, 4), (2, 6), (3, 2)] + late[:2] + last[0]
+    side = [(1, 0), (1, 2)] + late[2:] + last[1]
     order = lead + near + far + side
-    batches = [
-        [(0, 0)] + near,
-        lead,
-        [(2, 2), (2, 4)],
-        [(2, 6), (3, 2)],
-        [(1, 0), (1, 2)],
-        [(3, 4), (1, 4)],
-    ]
-    last = [(3, 6), (1, 6)]
+    batches = [[(0, 0)] + near, lead, [(2, 2), (2, 4)], [(2, 6), (3, 2)], [(1, 0), (1, 2)]]
     got = {}
-    sent = dict(zip(lead, pick(lead, bricks, weights, aperture, owners)))
+    sent = dict(zip(lead, pick(lead, single, bricks, weights, aperture, owners)))
     rest = [(0, 0)] + order[len(lead) :]
-    sent.update(zip(rest, pick(rest, bricks, weights, aperture, owners)))
+    sent.update(zip(rest, pick(rest, single, bricks, weights, aperture, owners)))
     got[0, 0] = sent[0, 0]
     for key in order:
         got[key] = permute(sent[key], *key)
@@ -410,11 +408,14 @@
         messages = [got[key] for key in batch]
         images = image_step(messages, None, images, columns, group)
     mine, other = images
-    late = [got[key] for key in last]
     other = permute(other, 0, 1)
-    relayed = permute(jnp.concatenate([m[SIDE:] for m in late], axis=0), 0, 1)
-    (mine,) = image_step(late, None, [mine], columns, group, sides=1)
-    image, _ = image_step([], relayed, [mine, other], columns, group, final=True, sides=1)
+    for batch in (late, last[0]):
+        messages = [got[key] for key in batch]
+        (mine,) = image_step(messages, None, [mine], columns, group, sides=1)
+    image, _ = image_step(
+        [got[key] for key in last[1]], None, [mine, other], columns, group,
+        final=True, sides=1,
+    )
     return image.reshape(group, 2 * SUB, FINE, 2 * BZ)
 
 

time: 88.4 us -> 84.9 us (0.960)
  waiting for transfers between devices: 39.4 us -> 13.1 us
  starting transfers between devices: 28.4 us -> 51.2 us
    ppermute x17 -> x20, waiting for transfers between devices: 39.4 us -> 13.1 us  [permute(): return lax.ppermute(value, ('src', 'tile'), pairs)]
    ppermute x17 -> x20, starting transfers between devices: 28.4 us -> 51.2 us  [permute(): return lax.ppermute(value, ('src', 'tile'), pairs)]
  transfers between devices with their start and end apart: 17 -> 20, of which waited for: 7 -> 5; matrix products, arithmetic and copies ran while one was open for 0% -> 0% of each run, Pallas kernels for 15% -> 17%
where the time goes in v5:
time: 84.9 us; the launch traced here: 84.7 us
  starting transfers between devices  51.2 us (60%)
  Pallas kernels  20.2 us (24%)
  waiting for transfers between devices  13.1 us (15%)
    ppermute x20, starting transfers between devices, permute(): return lax.ppermute(value, ('src', 'tile'), pairs)  51.2 us
    pallas_call x8, Pallas kernels, image_step(): pl.pallas_call(functools.partial(image_kernel, entries, rows, len(arrays)...  15.7 us
    ppermute x20, waiting for transfers between devices, permute(): return lax.ppermute(value, ('src', 'tile'), pairs)  13.1 us
    pallas_call x2, Pallas kernels, pick(): pl.pallas_call(functools.partial(pick_kernel, sends, quarters, group), ou...  4.52 us
  transfers between devices with their start and end apart: 20, of which 5 were waited for; matrix products, arithmetic and copies ran while one was open for 0% of the time, Pallas kernels for 17%

profile of v5, /device:TPU:0, one launch (start us, length us, event | category | flops | bytes accessed | tf_op | source)
XLA Modules:
  0.0 84.7 jit_solution(4020769511596666304)
XLA Ops:
  0.0 0.0 copy-start
  0.0 1.5 %shard_map.47 = (f32[41,8,128]{2,1,0:T(8,128)S(1)}, f32[41,8,128]{2,1,0:T(8,128)S(1)}) custom-call(s32[1,32]{1,0:T(1,128)} %mask_in.3, f32[1,32]{1,0:T(1,128)} %weight_in.3, f32[32,4,8,1024]{3,2,1,0:T(8,128)} %bitcast.2), custom_call_target="tpu_custom_call" | custom-call | tf_op jit(solution)/shard_map/pallas_call | solution.py:209
  1.5 4.1 %collective-permute-start.14 = (f32[41,8,128]{2,1,0:T(8,128)S(1)}, f32[41,8,128]{2,1,0:T(8,128)S(1)}, u32[]{:S(2)}, u32[]{:S(2)}) collective-permute-start(f32[41,8,128]{2,1,0:T(8,128)S(1)} %get-tuple-element.50), channel_id=1, source_target_pairs={{0,16},{1,17},{2,18},{3,19},{4,20},{5,21},{6,22},{7,23},{8,24},{9,... | collective-permute-start | bytes 503816 | tf_op jit(solution)/shard_map/ppermute | solution.py:387
  5.6 1.3 %collective-permute-start.15 = (f32[41,8,128]{2,1,0:T(8,128)S(1)}, f32[41,8,128]{2,1,0:T(8,128)S(1)}, u32[]{:S(2)}, u32[]{:S(2)}) collective-permute-start(f32[41,8,128]{2,1,0:T(8,128)S(1)} %get-tuple-element.51), channel_id=1, source_target_pairs={{0,24},{1,25},{2,26},{3,27},{4,28},{5,29},{6,30},{7,31},{8,16},{9,... | collective-permute-start | bytes 503816 | tf_op jit(solution)/shard_map/ppermute | solution.py:387
  7.0 3.0 %shard_map.46 = (f32[41,8,128]{2,1,0:T(8,128)S(1)}, f32[41,8,128]{2,1,0:T(8,128)S(1)}, f32[41,8,128]{2,1,0:T(8,128)S(1)}, f32[41,8,128]{2,1,0:T(8,128)S(1)}, f32...) custom-call(s32[1,32]{1,0:T(1,128)} %mask_in.3, ...), custom_call_target="tpu_custom_call" | custom-call | tf_op jit(solution)/shard_map/pallas_call | solution.py:209
  10.0 2.7 %collective-permute-start.12 = (f32[41,8,128]{2,1,0:T(8,128)S(1)}, f32[41,8,128]{2,1,0:T(8,128)S(1)}, u32[]{:S(2)}, u32[]{:S(2)}) collective-permute-start(f32[41,8,128]{2,1,0:T(8,128)S(1)} %get-tuple-element.48), channel_id=1, source_target_pairs={{0,18},{1,19},{2,16},{3,17},{4,22},{5,23},{6,20},{7,21},{8,26},{9,... | collective-permute-start | bytes 503816 | tf_op jit(solution)/shard_map/ppermute | solution.py:387
  12.7 0.5 collective-permute-start.16
  13.2 1.5 %collective-permute-start.17 = (f32[41,8,128]{2,1,0:T(8,128)S(1)}, f32[41,8,128]{2,1,0:T(8,128)S(1)}, u32[]{:S(2)}, u32[]{:S(2)}) collective-permute-start(f32[41,8,128]{2,1,0:T(8,128)S(1)} %get-tuple-element.54), channel_id=1, source_target_pairs={{0,4},{1,5},{2,6},{3,7},{4,0},{5,1},{6,2},{7,3},{8,12},{9,13},{10,... | collective-permute-start | bytes 503816 | tf_op jit(solution)/shard_map/ppermute | solution.py:387
  14.8 6.8 %collective-permute-done.14.refs_0_ = f32[41,8,128]{2,1,0:T(8,128)S(1)} collective-permute-done((f32[41,8,128]{2,1,0:T(8,128)S(1)}, f32[41,8,128]{2,1,0:T(8,128)S(1)}, u32[]{:S(2)}, u32[]{:S(2)}) %collective-permute-start.14) | collective-permute-done | bytes 167968 | tf_op jit(solution)/shard_map/ppermute | solution.py:387
  21.6 2.8 %collective-permute-start.18 = (f32[41,8,128]{2,1,0:T(8,128)S(1)}, f32[41,8,128]{2,1,0:T(8,128)S(1)}, u32[]{:S(2)}, u32[]{:S(2)}) collective-permute-start(f32[41,8,128]{2,1,0:T(8,128)S(1)} %get-tuple-element.55), channel_id=1, source_target_pairs={{0,6},{1,7},{2,4},{3,5},{4,2},{5,3},{6,0},{7,1},{8,14},{9,15},{10,... | collective-permute-start | bytes 503816 | tf_op jit(solution)/shard_map/ppermute | solution.py:387
  24.3 0.0 collective-permute-done.15.refs_1_
  24.3 3.7 %collective-permute-start.13 = (f32[41,8,128]{2,1,0:T(8,128)S(1)}, f32[41,8,128]{2,1,0:T(8,128)S(1)}, u32[]{:S(2)}, u32[]{:S(2)}) collective-permute-start(f32[41,8,128]{2,1,0:T(8,128)S(1)} %get-tuple-element.49), channel_id=1, source_target_pairs={{0,20},{1,21},{2,22},{3,23},{4,16},{5,17},{6,18},{7,19},{8,28},{9,... | collective-permute-start | bytes 503816 | tf_op jit(solution)/shard_map/ppermute | solution.py:387
  28.0 1.1 %collective-permute-done.12.refs_0_ = f32[41,8,128]{2,1,0:T(8,128)S(1)} collective-permute-done((f32[41,8,128]{2,1,0:T(8,128)S(1)}, f32[41,8,128]{2,1,0:T(8,128)S(1)}, u32[]{:S(2)}, u32[]{:S(2)}) %collective-permute-start.12) | collective-permute-done | bytes 167968 | tf_op jit(solution)/shard_map/ppermute | solution.py:387
  29.1 0.5 collective-permute-start.10
  29.6 0.0 collective-permute-done.16.refs_1_
  29.6 3.4 %collective-permute-start.11 = (f32[41,8,128]{2,1,0:T(8,128)S(1)}, f32[41,8,128]{2,1,0:T(8,128)S(1)}, u32[]{:S(2)}, u32[]{:S(2)}) collective-permute-start(f32[41,8,128]{2,1,0:T(8,128)S(1)} %get-tuple-element.47), channel_id=1, source_target_pairs={{0,26},{1,27},{2,24},{3,25},{4,30},{5,31},{6,28},{7,29},{8,18},{9,... | collective-permute-start | bytes 503816 | tf_op jit(solution)/shard_map/ppermute | solution.py:387
  32.9 0.0 collective-permute-done.17.refs_2_
  32.9 9.1 %collective-permute-start.8 = (f32[41,8,128]{2,1,0:T(8,128)S(1)}, f32[41,8,128]{2,1,0:T(8,128)S(1)}, u32[]{:S(2)}, u32[]{:S(2)}) collective-permute-start(f32[41,8,128]{2,1,0:T(8,128)S(1)} %get-tuple-element.44), channel_id=1, source_target_pairs={{0,8},{1,9},{2,10},{3,11},{4,12},{5,13},{6,14},{7,15},{8,0},{9,1},... | collective-permute-start | bytes 503816 | tf_op jit(solution)/shard_map/ppermute | solution.py:387
  42.0 0.0 collective-permute-done.18.refs_3_
  42.0 2.0 %collective-permute-start.9 = (f32[41,8,128]{2,1,0:T(8,128)S(1)}, f32[41,8,128]{2,1,0:T(8,128)S(1)}, u32[]{:S(2)}, u32[]{:S(2)}) collective-permute-start(f32[41,8,128]{2,1,0:T(8,128)S(1)} %get-tuple-element.45), channel_id=1, source_target_pairs={{0,10},{1,11},{2,8},{3,9},{4,14},{5,15},{6,12},{7,13},{8,2},{9,3},... | collective-permute-start | bytes 503816 | tf_op jit(solution)/shard_map/ppermute | solution.py:387
  44.0 0.0 copy-done
  44.0 3.0 %shard_map.48 = (f32[4,512,128]{2,1,0:T(8,128)S(1)}, f32[4,512,128]{2,1,0:T(8,128)S(1)}) custom-call(f32[41,8,128]{2,1,0:T(8,128)S(1)} %get-tuple-element.52.refs_0_, f32[41,8,128]{2,1,0:T(8,128)S(1)} %collective-permute-done.16.refs_1_, f32[41,8,128]{2,1,0:T(8,128)S(1)} %collective-permute-done.17.refs_2_, ...), custom_call_target="tpu_custom_call" | custom-call | tf_op jit(solution)/shard_map/pallas_call | solution.py:363
  47.0 1.8 %shard_map.49 = (f32[4,512,128]{2,1,0:T(8,128)S(1)}, f32[4,512,128]{2,1,0:T(8,128)S(1)}) custom-call(f32[41,8,128]{2,1,0:T(8,128)S(1)} %collective-permute-done.14.refs_0_, f32[41,8,128]{2,1,0:T(8,128)S(1)} %collective-permute-done.15.refs_1_, bf16[256,512]{1,0:T(8,128)(2,1)S(1)} %copy-done, ...), custom_call_target="tpu_custom_call", output_to_operand_aliasing={{0}: (3, {}), {1}: (4, {})} | custom-call | tf_op jit(solution)/shard_map/pallas_call | solution.py:363
  48.9 0.0 collective-permute-done.13.refs_1_
  48.9 1.8 %shard_map.50 = (f32[4,512,128]{2,1,0:T(8,128)S(1)}, f32[4,512,128]{2,1,0:T(8,128)S(1)}) custom-call(f32[41,8,128]{2,1,0:T(8,128)S(1)} %collective-permute-done.12.refs_0_, f32[41,8,128]{2,1,0:T(8,128)S(1)} %collective-permute-done.13.refs_1_, bf16[256,512]{1,0:T(8,128)(2,1)S(1)} %copy-done, ...), custom_call_target="tpu_custom_call", output_to_operand_aliasing={{0}: (3, {}), {1}: (4, {})} | custom-call | tf_op jit(solution)/shard_map/pallas_call | solution.py:363
  50.7 0.0 collective-permute-done.10.refs_0_
  50.7 0.0 collective-permute-done.11.refs_1_
  50.7 1.8 %shard_map.51 = (f32[4,512,128]{2,1,0:T(8,128)S(1)}, f32[4,512,128]{2,1,0:T(8,128)S(1)}) custom-call(f32[41,8,128]{2,1,0:T(8,128)S(1)} %collective-permute-done.10.refs_0_, f32[41,8,128]{2,1,0:T(8,128)S(1)} %collective-permute-done.11.refs_1_, bf16[256,512]{1,0:T(8,128)(2,1)S(1)} %copy-done, ...), custom_call_target="tpu_custom_call", output_to_operand_aliasing={{0}: (3, {}), {1}: (4, {})} | custom-call | tf_op jit(solution)/shard_map/pallas_call | solution.py:363
  52.6 0.0 collective-permute-done.8.refs_0_
  52.6 0.1 collective-permute-done.9.refs_1_
  52.7 1.8 %shard_map.52 = (f32[4,512,128]{2,1,0:T(8,128)S(1)}, f32[4,512,128]{2,1,0:T(8,128)S(1)}) custom-call(f32[41,8,128]{2,1,0:T(8,128)S(1)} %collective-permute-done.8.refs_0_, f32[41,8,128]{2,1,0:T(8,128)S(1)} %collective-permute-done.9.refs_1_, bf16[256,512]{1,0:T(8,128)(2,1)S(1)} %copy-done, ...), custom_call_target="tpu_custom_call", output_to_operand_aliasing={{0}: (3, {}), {1}: (4, {})} | custom-call | tf_op jit(solution)/shard_map/pallas_call | solution.py:363
  54.5 0.1 collective-permute-start.19
  54.6 3.4 %collective-permute-start.4 = (f32[21,8,128]{2,1,0:T(8,128)S(1)}, f32[21,8,128]{2,1,0:T(8,128)S(1)}, u32[]{:S(2)}, u32[]{:S(2)}) collective-permute-start(f32[21,8,128]{2,1,0:T(8,128)S(1)} %get-tuple-element.40), channel_id=1, source_target_pairs={{0,28},{1,29},{2,30},{3,31},{4,24},{5,25},{6,26},{7,27},{8,20},{9,... | collective-permute-start | bytes 258056 | tf_op jit(solution)/shard_map/ppermute | solution.py:387
  58.0 1.2 %collective-permute-start.5 = (f32[21,8,128]{2,1,0:T(8,128)S(1)}, f32[21,8,128]{2,1,0:T(8,128)S(1)}, u32[]{:S(2)}, u32[]{:S(2)}) collective-permute-start(f32[21,8,128]{2,1,0:T(8,128)S(1)} %get-tuple-element.41), channel_id=1, source_target_pairs={{0,29},{1,28},{2,31},{3,30},{4,25},{5,24},{6,27},{7,26},{8,21},{9,... | collective-permute-start | bytes 258056 | tf_op jit(solution)/shard_map/ppermute | solution.py:387
  59.2 1.2 %collective-permute-start.6 = (f32[21,8,128]{2,1,0:T(8,128)S(1)}, f32[21,8,128]{2,1,0:T(8,128)S(1)}, u32[]{:S(2)}, u32[]{:S(2)}) collective-permute-start(f32[21,8,128]{2,1,0:T(8,128)S(1)} %get-tuple-element.42), channel_id=1, source_target_pairs={{0,14},{1,15},{2,12},{3,13},{4,10},{5,11},{6,8},{7,9},{8,6},{9,7},... | collective-permute-start | bytes 258056 | tf_op jit(solution)/shard_map/ppermute | solution.py:387
  60.4 2.3 %collective-permute-start.7 = (f32[21,8,128]{2,1,0:T(8,128)S(1)}, f32[21,8,128]{2,1,0:T(8,128)S(1)}, u32[]{:S(2)}, u32[]{:S(2)}) collective-permute-start(f32[21,8,128]{2,1,0:T(8,128)S(1)} %get-tuple-element.43), channel_id=1, source_target_pairs={{0,15},{1,14},{2,13},{3,12},{4,11},{5,10},{6,9},{7,8},{8,7},{9,6},... | collective-permute-start | bytes 258056 | tf_op jit(solution)/shard_map/ppermute | solution.py:387
  62.7 0.0 collective-permute-done.4.refs_0_
  62.7 5.8 %collective-permute-start = (f32[21,8,128]{2,1,0:T(8,128)S(1)}, f32[21,8,128]{2,1,0:T(8,128)S(1)}, u32[]{:S(2)}, u32[]{:S(2)}) collective-permute-start(f32[21,8,128]{2,1,0:T(8,128)S(1)} %get-tuple-element.36), channel_id=1, source_target_pairs={{0,12},{1,13},{2,14},{3,15},{4,8},{5,9},{6,10},{7,11},{8,4},{9,5},... | collective-permute-start | bytes 258056 | tf_op jit(solution)/shard_map/ppermute | solution.py:387
  68.4 0.0 collective-permute-done.5.refs_1_
  68.4 4.2 %collective-permute-start.2 = (f32[21,8,128]{2,1,0:T(8,128)S(1)}, f32[21,8,128]{2,1,0:T(8,128)S(1)}, u32[]{:S(2)}, u32[]{:S(2)}) collective-permute-start(f32[21,8,128]{2,1,0:T(8,128)S(1)} %get-tuple-element.38), channel_id=1, source_target_pairs={{0,30},{1,31},{2,28},{3,29},{4,26},{5,27},{6,24},{7,25},{8,22},{9,... | collective-permute-start | bytes 258056 | tf_op jit(solution)/shard_map/ppermute | solution.py:387
  72.6 0.0 collective-permute-done.6.refs_2_
  72.7 0.0 collective-permute-start.3
  72.7 0.0 collective-permute-done.7.refs_3_
  72.7 1.6 %collective-permute-start.1 = (f32[21,8,128]{2,1,0:T(8,128)S(1)}, f32[21,8,128]{2,1,0:T(8,128)S(1)}, u32[]{:S(2)}, u32[]{:S(2)}) collective-permute-start(f32[21,8,128]{2,1,0:T(8,128)S(1)} %get-tuple-element.37), channel_id=1, source_target_pairs={{0,13},{1,12},{2,15},{3,14},{4,9},{5,8},{6,11},{7,10},{8,5},{9,4},... | collective-permute-start | bytes 258056 | tf_op jit(solution)/shard_map/ppermute | solution.py:387
  74.3 1.8 %shard_map.53.refs_3_ = f32[4,512,128]{2,1,0:T(8,128)S(1)} custom-call(f32[21,8,128]{2,1,0:T(8,128)S(1)} %collective-permute-done.4.refs_0_, f32[21,8,128]{2,1,0:T(8,128)S(1)} %collective-permute-done.5.refs_1_, f32[21,8,128]{2,1,0:T(8,128)S(1)} %collective-permute-done.6.refs_2_, ...), custom_call_target="tpu_custom_call", output_to_operand_aliasing={{}: (5, {})} | custom-call | tf_op jit(solution)/shard_map/pallas_call | solution.py:363
  76.1 0.6 collective-permute-done.2.refs_0_
  76.7 4.5 %collective-permute-done.3.refs_1_ = f32[21,8,128]{2,1,0:T(8,128)S(1)} collective-permute-done((f32[21,8,128]{2,1,0:T(8,128)S(1)}, f32[21,8,128]{2,1,0:T(8,128)S(1)}, u32[]{:S(2)}, u32[]{:S(2)}) %collective-permute-start.3) | collective-permute-done | bytes 86048 | tf_op jit(solution)/shard_map/ppermute | solution.py:387
  81.2 1.2 %shard_map.54.refs_3_ = f32[4,512,128]{2,1,0:T(8,128)S(1)} custom-call(f32[21,8,128]{2,1,0:T(8,128)S(1)} %collective-permute-done.2.refs_0_, f32[21,8,128]{2,1,0:T(8,128)S(1)} %collective-permute-done.3.refs_1_, bf16[256,512]{1,0:T(8,128)(2,1)S(1)} %copy-done, f32[4,512,128]{2,1,0:T(8,128)S(1)} %shard_map.53.refs_3_), custom_call_target="tpu_custom_call", output_to_operand_aliasing={{}: (3, {})} | custom-call | tf_op jit(solution)/shard_map/pallas_call | solution.py:363
  82.4 0.0 collective-permute-done.refs_0_
  82.4 0.0 collective-permute-done.1.refs_1_
  82.4 0.0 collective-permute-done.19.refs_4_
  82.5 2.3 %shard_map.55 = (f32[4,512,128]{2,1,0:T(8,128)}, f32[4,512,128]{2,1,0:T(8,128)S(1)}) custom-call(f32[21,8,128]{2,1,0:T(8,128)S(1)} %collective-permute-done.refs_0_, f32[21,8,128]{2,1,0:T(8,128)S(1)} %collective-permute-done.1.refs_1_, bf16[256,512]{1,0:T(8,128)(2,1)S(1)} %copy-done, ...), custom_call_target="tpu_custom_call", output_to_operand_aliasing={{1}: (3, {})} | custom-call | tf_op jit(solution)/shard_map/pallas_call | solution.py:363
Async XLA Ops:
  0.0 44.0 %copy-start = (bf16[256,512]{1,0:T(8,128)(2,1)S(1)}, bf16[256,512]{1,0:T(8,128)(2,1)}, u32[]{:S(2)}) copy-start(bf16[256,512]{1,0:T(8,128)(2,1)} %constant.2.clone.refs_4_.refs_2_) | copy-start | bytes 786436
  1.5 20.1 %collective-permute-start.14 = (f32[41,8,128]{2,1,0:T(8,128)S(1)}, f32[41,8,128]{2,1,0:T(8,128)S(1)}, u32[]{:S(2)}, u32[]{:S(2)}) collective-permute-start(f32[41,8,128]{2,1,0:T(8,128)S(1)} %get-tuple-element.50), channel_id=1, source_target_pairs={{0,16},{1,17},{2,18},{3,19},{4,20},{5,21},{6,22},{7,23},{8,24},{9,... | collective-permute-start | bytes 503816 | tf_op jit(solution)/shard_map/ppermute | solution.py:387
  5.6 18.7 %collective-permute-start.15 = (f32[41,8,128]{2,1,0:T(8,128)S(1)}, f32[41,8,128]{2,1,0:T(8,128)S(1)}, u32[]{:S(2)}, u32[]{:S(2)}) collective-permute-start(f32[41,8,128]{2,1,0:T(8,128)S(1)} %get-tuple-element.51), channel_id=1, source_target_pairs={{0,24},{1,25},{2,26},{3,27},{4,28},{5,29},{6,30},{7,31},{8,16},{9,... | collective-permute-start | bytes 503816 | tf_op jit(solution)/shard_map/ppermute | solution.py:387
  10.0 19.0 %collective-permute-start.12 = (f32[41,8,128]{2,1,0:T(8,128)S(1)}, f32[41,8,128]{2,1,0:T(8,128)S(1)}, u32[]{:S(2)}, u32[]{:S(2)}) collective-permute-start(f32[41,8,128]{2,1,0:T(8,128)S(1)} %get-tuple-element.48), channel_id=1, source_target_pairs={{0,18},{1,19},{2,16},{3,17},{4,22},{5,23},{6,20},{7,21},{8,26},{9,... | collective-permute-start | bytes 503816 | tf_op jit(solution)/shard_map/ppermute | solution.py:387
  12.7 16.9 %collective-permute-start.16 = (f32[41,8,128]{2,1,0:T(8,128)S(1)}, f32[41,8,128]{2,1,0:T(8,128)S(1)}, u32[]{:S(2)}, u32[]{:S(2)}) collective-permute-start(f32[41,8,128]{2,1,0:T(8,128)S(1)} %get-tuple-element.53), channel_id=1, source_target_pairs={{0,2},{1,3},{2,0},{3,1},{4,6},{5,7},{6,4},{7,5},{8,10},{9,11},{10,... | collective-permute-start | bytes 503816 | tf_op jit(solution)/shard_map/ppermute | solution.py:387
  13.2 19.7 %collective-permute-start.17 = (f32[41,8,128]{2,1,0:T(8,128)S(1)}, f32[41,8,128]{2,1,0:T(8,128)S(1)}, u32[]{:S(2)}, u32[]{:S(2)}) collective-permute-start(f32[41,8,128]{2,1,0:T(8,128)S(1)} %get-tuple-element.54), channel_id=1, source_target_pairs={{0,4},{1,5},{2,6},{3,7},{4,0},{5,1},{6,2},{7,3},{8,12},{9,13},{10,... | collective-permute-start | bytes 503816 | tf_op jit(solution)/shard_map/ppermute | solution.py:387
  21.6 20.4 %collective-permute-start.18 = (f32[41,8,128]{2,1,0:T(8,128)S(1)}, f32[41,8,128]{2,1,0:T(8,128)S(1)}, u32[]{:S(2)}, u32[]{:S(2)}) collective-permute-start(f32[41,8,128]{2,1,0:T(8,128)S(1)} %get-tuple-element.55), channel_id=1, source_target_pairs={{0,6},{1,7},{2,4},{3,5},{4,2},{5,3},{6,0},{7,1},{8,14},{9,15},{10,... | collective-permute-start | bytes 503816 | tf_op jit(solution)/shard_map/ppermute | solution.py:387
  24.3 24.5 %collective-permute-start.13 = (f32[41,8,128]{2,1,0:T(8,128)S(1)}, f32[41,8,128]{2,1,0:T(8,128)S(1)}, u32[]{:S(2)}, u32[]{:S(2)}) collective-permute-start(f32[41,8,128]{2,1,0:T(8,128)S(1)} %get-tuple-element.49), channel_id=1, source_target_pairs={{0,20},{1,21},{2,22},{3,23},{4,16},{5,17},{6,18},{7,19},{8,28},{9,... | collective-permute-start | bytes 503816 | tf_op jit(solution)/shard_map/ppermute | solution.py:387
  29.1 21.7 %collective-permute-start.10 = (f32[41,8,128]{2,1,0:T(8,128)S(1)}, f32[41,8,128]{2,1,0:T(8,128)S(1)}, u32[]{:S(2)}, u32[]{:S(2)}) collective-permute-start(f32[41,8,128]{2,1,0:T(8,128)S(1)} %get-tuple-element.46), channel_id=1, source_target_pairs={{0,22},{1,23},{2,20},{3,21},{4,18},{5,19},{6,16},{7,17},{8,30},{9,... | collective-permute-start | bytes 503816 | tf_op jit(solution)/shard_map/ppermute | solution.py:387
  29.6 21.2 %collective-permute-start.11 = (f32[41,8,128]{2,1,0:T(8,128)S(1)}, f32[41,8,128]{2,1,0:T(8,128)S(1)}, u32[]{:S(2)}, u32[]{:S(2)}) collective-permute-start(f32[41,8,128]{2,1,0:T(8,128)S(1)} %get-tuple-element.47), channel_id=1, source_target_pairs={{0,26},{1,27},{2,24},{3,25},{4,30},{5,31},{6,28},{7,29},{8,18},{9,... | collective-permute-start | bytes 503816 | tf_op jit(solution)/shard_map/ppermute | solution.py:387
  32.9 19.7 %collective-permute-start.8 = (f32[41,8,128]{2,1,0:T(8,128)S(1)}, f32[41,8,128]{2,1,0:T(8,128)S(1)}, u32[]{:S(2)}, u32[]{:S(2)}) collective-permute-start(f32[41,8,128]{2,1,0:T(8,128)S(1)} %get-tuple-element.44), channel_id=1, source_target_pairs={{0,8},{1,9},{2,10},{3,11},{4,12},{5,13},{6,14},{7,15},{8,0},{9,1},... | collective-permute-start | bytes 503816 | tf_op jit(solution)/shard_map/ppermute | solution.py:387
  42.0 10.7 %collective-permute-start.9 = (f32[41,8,128]{2,1,0:T(8,128)S(1)}, f32[41,8,128]{2,1,0:T(8,128)S(1)}, u32[]{:S(2)}, u32[]{:S(2)}) collective-permute-start(f32[41,8,128]{2,1,0:T(8,128)S(1)} %get-tuple-element.45), channel_id=1, source_target_pairs={{0,10},{1,11},{2,8},{3,9},{4,14},{5,15},{6,12},{7,13},{8,2},{9,3},... | collective-permute-start | bytes 503816 | tf_op jit(solution)/shard_map/ppermute | solution.py:387
  54.5 27.9 %collective-permute-start.19 = (f32[4,512,128]{2,1,0:T(8,128)S(1)}, f32[4,512,128]{2,1,0:T(8,128)S(1)}, u32[]{:S(2)}, u32[]{:S(2)}) collective-permute-start(f32[4,512,128]{2,1,0:T(8,128)S(1)} %get-tuple-element.65), channel_id=1, source_target_pairs={{0,1},{1,0},{2,3},{3,2},{4,5},{5,4},{6,7},{7,6},{8,9},{9,8},{10,11... | collective-permute-start | bytes 3145736 | tf_op jit(solution)/shard_map/ppermute | solution.py:387
  54.6 8.1 %collective-permute-start.4 = (f32[21,8,128]{2,1,0:T(8,128)S(1)}, f32[21,8,128]{2,1,0:T(8,128)S(1)}, u32[]{:S(2)}, u32[]{:S(2)}) collective-permute-start(f32[21,8,128]{2,1,0:T(8,128)S(1)} %get-tuple-element.40), channel_id=1, source_target_pairs={{0,28},{1,29},{2,30},{3,31},{4,24},{5,25},{6,26},{7,27},{8,20},{9,... | collective-permute-start | bytes 258056 | tf_op jit(solution)/shard_map/ppermute | solution.py:387
  58.0 10.5 %collective-permute-start.5 = (f32[21,8,128]{2,1,0:T(8,128)S(1)}, f32[21,8,128]{2,1,0:T(8,128)S(1)}, u32[]{:S(2)}, u32[]{:S(2)}) collective-permute-start(f32[21,8,128]{2,1,0:T(8,128)S(1)} %get-tuple-element.41), channel_id=1, source_target_pairs={{0,29},{1,28},{2,31},{3,30},{4,25},{5,24},{6,27},{7,26},{8,21},{9,... | collective-permute-start | bytes 258056 | tf_op jit(solution)/shard_map/ppermute | solution.py:387
  59.2 13.5 %collective-permute-start.6 = (f32[21,8,128]{2,1,0:T(8,128)S(1)}, f32[21,8,128]{2,1,0:T(8,128)S(1)}, u32[]{:S(2)}, u32[]{:S(2)}) collective-permute-start(f32[21,8,128]{2,1,0:T(8,128)S(1)} %get-tuple-element.42), channel_id=1, source_target_pairs={{0,14},{1,15},{2,12},{3,13},{4,10},{5,11},{6,8},{7,9},{8,6},{9,7},... | collective-permute-start | bytes 258056 | tf_op jit(solution)/shard_map/ppermute | solution.py:387
  60.4 12.3 %collective-permute-start.7 = (f32[21,8,128]{2,1,0:T(8,128)S(1)}, f32[21,8,128]{2,1,0:T(8,128)S(1)}, u32[]{:S(2)}, u32[]{:S(2)}) collective-permute-start(f32[21,8,128]{2,1,0:T(8,128)S(1)} %get-tuple-element.43), channel_id=1, source_target_pairs={{0,15},{1,14},{2,13},{3,12},{4,11},{5,10},{6,9},{7,8},{8,7},{9,6},... | collective-permute-start | bytes 258056 | tf_op jit(solution)/shard_map/ppermute | solution.py:387
  62.7 19.7 %collective-permute-start = (f32[21,8,128]{2,1,0:T(8,128)S(1)}, f32[21,8,128]{2,1,0:T(8,128)S(1)}, u32[]{:S(2)}, u32[]{:S(2)}) collective-permute-start(f32[21,8,128]{2,1,0:T(8,128)S(1)} %get-tuple-element.36), channel_id=1, source_target_pairs={{0,12},{1,13},{2,14},{3,15},{4,8},{5,9},{6,10},{7,11},{8,4},{9,5},... | collective-permute-start | bytes 258056 | tf_op jit(solution)/shard_map/ppermute | solution.py:387
  68.4 8.3 %collective-permute-start.2 = (f32[21,8,128]{2,1,0:T(8,128)S(1)}, f32[21,8,128]{2,1,0:T(8,128)S(1)}, u32[]{:S(2)}, u32[]{:S(2)}) collective-permute-start(f32[21,8,128]{2,1,0:T(8,128)S(1)} %get-tuple-element.38), channel_id=1, source_target_pairs={{0,30},{1,31},{2,28},{3,29},{4,26},{5,27},{6,24},{7,25},{8,22},{9,... | collective-permute-start | bytes 258056 | tf_op jit(solution)/shard_map/ppermute | solution.py:387
  72.7 8.6 %collective-permute-start.3 = (f32[21,8,128]{2,1,0:T(8,128)S(1)}, f32[21,8,128]{2,1,0:T(8,128)S(1)}, u32[]{:S(2)}, u32[]{:S(2)}) collective-permute-start(f32[21,8,128]{2,1,0:T(8,128)S(1)} %get-tuple-element.39), channel_id=1, source_target_pairs={{0,31},{1,30},{2,29},{3,28},{4,27},{5,26},{6,25},{7,24},{8,23},{9,... | collective-permute-start | bytes 258056 | tf_op jit(solution)/shard_map/ppermute | solution.py:387
  72.7 9.8 %collective-permute-start.1 = (f32[21,8,128]{2,1,0:T(8,128)S(1)}, f32[21,8,128]{2,1,0:T(8,128)S(1)}, u32[]{:S(2)}, u32[]{:S(2)}) collective-permute-start(f32[21,8,128]{2,1,0:T(8,128)S(1)} %get-tuple-element.37), channel_id=1, source_target_pairs={{0,13},{1,12},{2,15},{3,14},{4,9},{5,8},{6,11},{7,10},{8,5},{9,4},... | collective-permute-start | bytes 258056 | tf_op jit(solution)/shard_map/ppermute | solution.py:387
